TPU v7x, 32 devices: a whole 2x2x4 slice. The times are simulated.
32 devices in a mesh: pa: 8 (over z, x), gz: 4 (over y, core).
Axes of the slice: x: 2, y: 2, z: 4, core: 2. Of those that a mesh axis runs over, the one named last changes fastest.
Arguments:
- source: float32 [32, 768, 768], P('gz', 'pa'), may hold values from -24 to 24
- cell_width: float32 [32], P('gz'), may hold values from 0.5 to 2
Outputs:
- potential: float32 [32, 768, 768], P('gz', 'pa')
All inputs are finite; a program needn't handle non-finite values.
Results may differ from a plain program's by a relative error of at most 0.00085.
Values sent between devices are 32-bit elements; how exact they have to be, the bound alone decides.
A program may use at most 64 MiB of HBM per device.

v0:
```python
import jax
import jax.numpy as jnp
import numpy as np
from jax import lax
from jax.experimental import pallas as pl
from jax.experimental.pallas import tpu as pltpu
from jax.sharding import PartitionSpec as P

HIGH = lax.Precision.HIGH


def summed_angles(width, coarse, fine, sine):
    f32 = lambda x: jnp.asarray(x.astype(np.float32))
    ca, sa = f32(np.cos(coarse))[:, None, :], f32(np.sin(coarse))[:, None, :]
    cb, sb = f32(np.cos(fine))[None, :, :], f32(np.sin(fine))[None, :, :]
    table = sa * cb + ca * sb if sine else ca * cb - sa * sb
    return table.reshape(width, width)


def split_steps(width):
    step = next(b for b in (32, 16, 8, 1) if width % b == 0)
    return np.arange(0, width, step, dtype=np.int64)[:, None], np.arange(step, dtype=np.int64)[:, None]


def cosine_table(width):
    odd = 2 * np.arange(width, dtype=np.int64)[None, :] + 1
    a, b = (k * odd % (4 * width) * (np.pi / (2 * width)) for k in split_steps(width))
    first = jnp.arange(width)[:, None] == 0
    weights = jnp.where(first, np.sqrt(1.0 / width), np.sqrt(2.0 / width)).astype(jnp.float32)
    return weights * summed_angles(width, a, b, False)


def sine_table(width):
    j = np.arange(1, width + 1, dtype=np.int64)[None, :]
    coarse, fine = split_steps(width)
    a, b = (l * j % (2 * (width + 1)) * (np.pi / (width + 1)) for l in (coarse, fine + 1))
    return np.float32(np.sqrt(2.0 / (width + 1))) * summed_angles(width, a, b, True)


def eigen_first(offset, count, width):
    values = 4.0 * np.sin(np.arange(width) * (np.pi / (2 * width))) ** 2
    return lax.dynamic_slice_in_dim(jnp.asarray(values, jnp.float32), offset, count)[:, None]


def eigen_second(width):
    values = 4.0 * np.sin(np.arange(1, width + 1) * (np.pi / (2 * (width + 1)))) ** 2
    return jnp.asarray(values, jnp.float32)[None, :]


def tiles(rows, width, body):
    lanes = 256 if width % 256 == 0 else width

    if rows % 8:
        for c in range(0, width, lanes):
            body(slice(0, rows), pl.ds(c, lanes))
        return

    def step(r, carry):
        row = pl.ds(pl.multiple_of(r * 8, 8), 8)
        for c in range(0, width, lanes):
            body(row, pl.ds(c, lanes))
        return carry

    lax.fori_loop(0, rows // 8, step, 0)


def ends_kernel(coef, ex, ey, spectral, ends):
    depth, rows, width = spectral.shape

    def body(row, col):
        eigen = ex[row, :] + ey[:, col]
        diag = [coef[0, z] + coef[1, z] + coef[2, z] * eigen for z in range(depth)]
        force = [coef[2, z] * spectral[z, row, col] for z in range(depth)]
        inverse = 1.0 / diag[0]
        value = force[0] * inverse
        other = 1.0 / diag[depth - 1]
        front = force[depth - 1] * other
        for z in range(1, depth):
            inverse = 1.0 / (diag[z] - (coef[0, z] * coef[1, z - 1]) * inverse)
            value = (force[z] + coef[0, z] * value) * inverse
            y = depth - 1 - z
            other = 1.0 / (diag[y] - (coef[1, y] * coef[0, y + 1]) * other)
            front = (force[y] + coef[1, y] * front) * other
        ends[0, row, col] = front
        ends[1, row, col] = value

    tiles(rows, width, body)


def reduced_kernel(coef, ex, ey, ends, sides):
    blocks = ends.shape[0] // 2
    rows, width = ends.shape[1:]
    depth = coef.shape[1] // blocks

    def body(row, col):
        eigen = ex[row, :] + ey[:, col]
        p = jnp.zeros_like(eigen)
        q = jnp.zeros_like(eigen)
        saved = []
        for b in range(blocks):
            s = b * depth
            diag = [coef[0, s + z] + coef[1, s + z] + coef[2, s + z] * eigen for z in range(depth)]
            inverse = 1.0 / diag[0]
            v1 = coef[0, s] * inverse
            other = 1.0 / diag[depth - 1]
            w0 = coef[1, s + depth - 1] * other
            for z in range(1, depth):
                inverse = 1.0 / (diag[z] - (coef[0, s + z] * coef[1, s + z - 1]) * inverse)
                v1 = v1 * (coef[0, s + z] * inverse)
                y = depth - 1 - z
                other = 1.0 / (diag[y] - (coef[1, s + y] * coef[0, s + y + 1]) * other)
                w0 = w0 * (coef[1, s + y] * other)
            w1 = coef[1, s + depth - 1] * inverse
            v0 = coef[0, s] * other
            scale = 1.0 / (1.0 - v0 * q)
            a = (ends[2 * b, row, col] + v0 * p) * scale
            c = w0 * scale
            p, q = ends[2 * b + 1, row, col] + v1 * (p + q * a), v1 * q * c + w1
            saved.append((a, c, p, q))
        head = jnp.zeros_like(eigen)
        for b in reversed(range(blocks)):
            a, c, p, q = saved[b]
            sides[2 * b + 1, row, col] = head
            if b + 1 < blocks:
                sides[2 * b + 2, row, col] = p + q * head
            head = a + c * head
        sides[0, row, col] = jnp.zeros_like(eigen)

    tiles(rows, width, body)


def final_kernel(coef, ex, ey, spectral, sides, solved):
    depth, rows, width = spectral.shape

    def body(row, col):
        eigen = ex[row, :] + ey[:, col]
        ratios, values = [], []
        for z in range(depth):
            diag = coef[0, z] + coef[1, z] + coef[2, z] * eigen
            force = coef[2, z] * spectral[z, row, col]
            if z == 0:
                force = force + coef[0, z] * sides[0, row, col]
            else:
                diag = diag - coef[0, z] * ratios[-1]
                force = force + coef[0, z] * values[-1]
            if z == depth - 1:
                force = force + coef[1, z] * sides[1, row, col]
            inverse = 1.0 / diag
            ratios.append(coef[1, z] * inverse)
            values.append(force * inverse)
        x = values[-1]
        solved[depth - 1, row, col] = x
        for z in reversed(range(depth - 1)):
            x = values[z] + ratios[z] * x
            solved[z, row, col] = x

    tiles(rows, width, body)


def solve_call(kernel, leads, lead_out, coef, ex, ey, *planes):
    rows, width = planes[0].shape[1:]
    block = next((b for b in (32, 24, 16, 8) if rows % b == 0), rows)
    spec = lambda lead: pl.BlockSpec((lead, block, width), lambda i: (0, i, 0))
    return pl.pallas_call(
        kernel,
        grid=(rows // block,),
        in_specs=[
            pl.BlockSpec(memory_space=pltpu.SMEM),
            pl.BlockSpec((block, 1), lambda i: (i, 0)),
            pl.BlockSpec((1, width), lambda i: (0, 0)),
        ]
        + [spec(lead) for lead in leads],
        out_specs=spec(lead_out),
        out_shape=jax.ShapeDtypeStruct((lead_out, rows, width), jnp.float32),
    )(coef, ex, ey, *planes)


def on_device(source, cell_width):
    depth, rows_local, width_x = source.shape
    blocks = lax.axis_size("gz")
    width_y = rows_local * lax.axis_size("pa")
    cos_table = cosine_table(width_x)
    sin_table = sine_table(width_y)
    block = lax.axis_index("gz")
    widths = lax.all_gather(cell_width, "gz", tiled=True)
    padded = jnp.pad(widths, 1)
    coef = jnp.stack(
        [2.0 / (padded[:-2] + widths), 2.0 / (widths + padded[2:]), widths]
    )
    own = lax.dynamic_slice_in_dim(coef, block * depth, depth, axis=1)
    along_x = jnp.einsum("zyi,ki->zky", source, cos_table, precision=HIGH)
    spectral = jnp.einsum(
        "zkj,lj->zkl",
        lax.all_to_all(along_x, "pa", split_axis=1, concat_axis=2, tiled=True),
        sin_table,
        precision=HIGH,
    )
    kx = spectral.shape[1]
    first = lax.axis_index("pa") * kx
    part = kx // blocks
    ex = eigen_first(first, kx, width_x)
    ex_part = eigen_first(first + block * part, part, width_x)
    ey = eigen_second(width_y)
    ends = solve_call(ends_kernel, (depth,), 2, own, ex, ey, spectral)
    ends = lax.all_to_all(ends, "gz", split_axis=1, concat_axis=0, tiled=True)
    sides = solve_call(reduced_kernel, (2 * blocks,), 2 * blocks, coef, ex_part, ey, ends)
    sides = lax.all_to_all(sides, "gz", split_axis=0, concat_axis=1, tiled=True)
    solved = solve_call(final_kernel, (depth, 2), depth, own, ex, ey, spectral, sides)
    along_y = jnp.einsum("zkl,lj->zkj", solved, sin_table, precision=HIGH)
    return jnp.einsum(
        "zky,ki->zyi",
        lax.all_to_all(along_y, "pa", split_axis=2, concat_axis=1, tiled=True),
        cos_table,
        precision=HIGH,
    )


def solution(mesh):
    in_specs = (P("gz", "pa", None), P("gz"))
    out_specs = P("gz", "pa", None)
    return jax.shard_map(
        on_device, mesh=mesh, in_specs=in_specs, out_specs=out_specs, check_vma=False
    )
```

profile of v0, /device:TPU:0, one launch (start us, length us, event | category | flops | bytes accessed | tf_op | source)
XLA Modules:
  0.0 248.3 jit_solution(1028681436258444491)
XLA Ops:
  0.0 0.0 copy-start
  0.0 3.0 %broadcast_multiply_fusion = (f32[24,32,768]{2,1,0:T(8,128)}, f32[24,32,768]{2,1,0:T(8,128)S(1)}) fusion(f32[24,32]{1,0:T(8,128)S(1)} %fusion.5, f32[32,768]{1,0:T(8,128)} %constant.56.clone, f32[24,768]{1,0:T(8,128)} %constant.54.clone, f32[32,768]{1,0:T(8,128)} %constant.55.clone, f32[24,768]{1,0:T(8,128)} %constant.53.clone), kind=kLoop, calls=%fused_computation.8 | loop fusion | flops 2359296 | bytes 5065728 | tf_op jit(solution)/shard_map/mul | solution.py:30
  3.1 0.2 bitcast_multiply_fusion
  3.3 0.0 copy-done
  3.3 4.4 %fusion.2 = f32[8,768,96]{1,2,0:T(8,128)} fusion(f32[8,96,768]{2,1,0:T(8,128)S(1)} %copy-done, f32[768,768]{1,0:T(8,128)S(1)} %bitcast_multiply_fusion), kind=kOutput, calls=%fused_computation.7 | convolution fusion | flops 2717908992 | bytes 7077888 | tf_op jit(solution)/shard_map/zyi,ki->zky/dot_general | solution.py:191
  7.7 3.4 %copy.21 = f32[8,768,96]{2,0,1:T(8,128)} copy(f32[8,768,96]{1,2,0:T(8,128)} %fusion.2) | data formatting | bytes 4718592 | tf_op jit(solution)/shard_map/zyi,ki->zky/transpose | solution.py:191
  11.1 0.0 copy-start.7
  11.1 0.0 copy-start.6
  11.1 0.0 copy-start.3
  11.1 0.0 copy-start.4
  11.1 7.4 %all-to-all-start = ((f32[8,768,96]{2,0,1:T(8,128)}), f32[8,768,96]{2,0,1:T(8,128)}, u32[]{:S(2)}, u32[]{:S(2)}) async-start(f32[8,768,96]{2,0,1:T(8,128)} %copy.21), calls=%async_computation | async-start | bytes 6291456 | tf_op jit(solution)/shard_map/all_to_all | solution.py:194
  18.6 0.8 dynamic-slice_bitcast_fusion.1
  19.3 0.7 copy.28.ex
  20.1 0.0 copy-done.7
  20.1 0.6 dynamic-slice
  21.3 0.0 copy-done.6
  21.3 0.2 dynamic-update-slice
  21.6 6.7 %all-reduce.1 = f32[32]{0:T(128)S(1)} all-reduce(f32[32]{0:T(128)S(1)} %dynamic-update-slice), channel_id=1, replica_groups=mesh['pa'=8,'gz'=4] {'gz'}, use_global_device_ids=true, to_apply=%add.1 | all-reduce | flops 32 | bytes 256
  28.3 0.1 divide_bitcast_fusion.1
  28.3 0.0 copy-start.5
  28.4 0.7 constant_dynamic-slice_fusion.coef
  29.0 0.0 copy-done.1
  29.0 0.0 copy-done.2
  29.0 0.0 copy-done.3
  29.0 0.0 copy-done.4
  29.0 1.8 add_multiply_fusion
  30.9 58.5 %all-to-all-done = f32[8,768,96]{2,0,1:T(8,128)} async-done(((f32[8,768,96]{2,0,1:T(8,128)}), f32[8,768,96]{2,0,1:T(8,128)}, u32[]{:S(2)}, u32[]{:S(2)}) %all-to-all-start) | async-done | bytes 2359328 | tf_op jit(solution)/shard_map/all_to_all | solution.py:194
  89.4 5.4 %copy.34 = f32[8,8,96,96]{3,1,2,0:T(8,128)} copy(f32[8,8,96,96]{3,0,2,1:T(8,128)} %bitcast.8) | data formatting | bytes 4718592 | tf_op jit(solution)/shard_map/all_to_all | solution.py:194
  94.8 0.0 copy-done.5
  94.8 4.4 %all_to_all.55 = f32[8,96,768]{2,1,0:T(8,128)} reshape(f32[8,96,8,96]{3,2,1,0:T(8,128)} %bitcast.57) | data formatting | bytes 4718592 | tf_op jit(solution)/shard_map/all_to_all | solution.py:194
  99.2 6.8 %fusion.7.spectral = f32[8,96,768]{2,1,0:T(8,128)} fusion(f32[8,96,768]{2,1,0:T(8,128)} %all_to_all.55, f32[768,768,1]{1,0,2:T(8,128)} %bitcast.54), kind=kOutput, calls=%fused_computation.19 | convolution fusion | flops 2717908992 | bytes 7077888 | tf_op jit(solution)/shard_map/zkj,lj->zkl/dot_general | solution.py:192
  106.0 4.5 %shard_map.127 = f32[2,96,768]{2,1,0:T(8,128)} custom-call(f32[3,8]{1,0:T(4,128)} %constant_dynamic-slice_fusion.coef, f32[96,1]{1,0:T(8,128)} %copy.28.ex, f32[1,768]{1,0:T(1,128)} %constant.65.ey, f32[8,96,768]{2,1,0:T(8,128)} %fusion.7.spectral), custom_call_target="tpu_custom_call" | custom-call | tf_op jit(solution)/shard_map/pallas_call | solution.py:164
  110.5 2.4 copy.24
  112.9 3.7 %all-to-all-start.1 = ((f32[2,96,768]{2,0,1:T(2,128)}), f32[2,96,768]{2,0,1:T(2,128)S(1)}, u32[]{:S(2)}, u32[]{:S(2)}) async-start(f32[2,96,768]{2,0,1:T(2,128)} %copy.24), calls=%async_computation.1 | async-start | bytes 1179648 | tf_op jit(solution)/shard_map/all_to_all | solution.py:205
  116.6 0.8 dynamic-slice_bitcast_fusion
  117.3 0.7 copy.26.ex
  118.0 7.8 %all-to-all-done.1 = f32[2,96,768]{2,0,1:T(2,128)S(1)} async-done(((f32[2,96,768]{2,0,1:T(2,128)}), f32[2,96,768]{2,0,1:T(2,128)S(1)}, u32[]{:S(2)}, u32[]{:S(2)}) %all-to-all-start.1) | async-done | bytes 589856 | tf_op jit(solution)/shard_map/all_to_all | solution.py:205
  125.9 0.9 copy.25
  126.7 3.5 %shard_map.128 = f32[8,24,768]{2,1,0:T(8,128)} custom-call(f32[3,32]{1,0:T(4,128)} %copy-done.5, f32[24,1]{1,0:T(8,128)} %copy.26.ex, f32[1,768]{1,0:T(1,128)} %constant.65.ey, f32[8,24,768]{2,1,0:T(8,128)} %bitcast.62), custom_call_target="tpu_custom_call" | custom-call | tf_op jit(solution)/shard_map/pallas_call | solution.py:164
  130.2 13.0 %all_to_all.72 = f32[8,24,768]{2,1,0:T(8,128)S(1)} all-to-all(f32[8,24,768]{2,1,0:T(8,128)} %shard_map.128), channel_id=1, replica_groups=mesh['pa'=8,'gz'=4] {'gz'}, dimensions={0} | all-to-all | bytes 1179648 | tf_op jit(solution)/shard_map/all_to_all | solution.py:207
  143.2 0.9 copy.27
  144.0 4.9 %shard_map.129 = f32[8,96,768]{2,1,0:T(8,128)} custom-call(f32[3,8]{1,0:T(4,128)} %constant_dynamic-slice_fusion.coef, f32[96,1]{1,0:T(8,128)} %copy.28.ex, f32[1,768]{1,0:T(1,128)} %constant.65.ey, f32[8,96,768]{2,1,0:T(8,128)} %fusion.7.spectral, f32[2,96,768]{2,1,0:T(8,128)} %bitcast.60), custom_call_target="tpu_custom_call" | custom-call | tf_op jit(solution)/shard_map/pallas_call | solution.py:164
  148.9 6.9 %fusion.8 = f32[8,96,768]{2,1,0:T(8,128)} fusion(f32[8,96,768]{2,1,0:T(8,128)} %shard_map.129, f32[768,768,1]{1,0,2:T(8,128)} %bitcast.55), kind=kOutput, calls=%fused_computation.20 | convolution fusion | flops 2717908992 | bytes 7077888 | tf_op jit(solution)/shard_map/zkl,lj->zkj/dot_general | solution.py:209
  155.8 3.4 %copy.29 = f32[8,96,768]{1,0,2:T(8,128)} copy(f32[8,96,768]{2,1,0:T(8,128)} %fusion.8) | data formatting | bytes 4718592 | tf_op jit(solution)/shard_map/zkl,lj->zkj/dot_general | solution.py:209
  159.2 74.4 %all_to_all.73 = f32[8,96,768]{1,0,2:T(8,128)S(1)} all-to-all(f32[8,96,768]{1,0,2:T(8,128)} %copy.29), channel_id=1, replica_groups=mesh['pa'=8,'gz'=4] {'pa'}, dimensions={2} | all-to-all | bytes 4718592 | tf_op jit(solution)/shard_map/all_to_all | solution.py:212
  233.7 3.4 %copy.33 = f32[8,96,8,96]{1,2,3,0:T(8,128)} copy(f32[8,96,8,96]{1,0,3,2:T(8,128)S(1)} %bitcast.56) | data formatting | bytes 4718592 | tf_op jit(solution)/shard_map/all_to_all | solution.py:212
  237.1 4.4 %all_to_all.67 = f32[8,768,96]{1,2,0:T(8,128)} reshape(f32[8,8,96,96]{2,1,3,0:T(8,128)} %bitcast.58) | data formatting | bytes 4718592 | tf_op jit(solution)/shard_map/all_to_all | solution.py:212
  241.5 6.8 %fusion.9 = f32[8,96,768]{2,1,0:T(8,128)} fusion(f32[8,768,96]{1,2,0:T(8,128)} %all_to_all.67, f32[768,768,1]{1,0,2:T(8,128)} %bitcast.59), kind=kOutput, calls=%fused_computation.21 | convolution fusion | flops 2717908992 | bytes 7077888 | tf_op jit(solution)/shard_map/zky,ki->zyi/dot_general | solution.py:210
  (6 shorter events, 0.0 us)
Async XLA Ops:
  0.0 3.3 %copy-start = (f32[8,96,768]{2,1,0:T(8,128)S(1)}, f32[8,96,768]{2,1,0:T(8,128)}, u32[]{:S(2)}) copy-start(f32[8,96,768]{2,1,0:T(8,128)} %param.13) | copy-start | bytes 7077892
  11.1 9.0 %copy-start.7 = (u32[32]{0:T(128)S(1)}, u32[32]{0:T(128)}, u32[]{:S(2)}) copy-start(u32[32]{0:T(128)} %constant.68) | copy-start | bytes 388
  11.1 10.2 %copy-start.6 = (f32[8]{0:T(128)S(1)}, f32[8]{0:T(128)}, u32[]{:S(2)}) copy-start(f32[8]{0:T(128)} %param.14) | copy-start | bytes 100
  11.1 17.9 %copy-start.1 = (f32[32,768]{1,0:T(8,128)S(1)}, f32[32,768]{1,0:T(8,128)}, u32[]{:S(2)}) copy-start(f32[32,768]{1,0:T(8,128)} %constant.59.clone) | copy-start | bytes 294916
  11.1 17.9 %copy-start.2 = (f32[32,768]{1,0:T(8,128)S(1)}, f32[32,768]{1,0:T(8,128)}, u32[]{:S(2)}) copy-start(f32[32,768]{1,0:T(8,128)} %constant.60.clone) | copy-start | bytes 294916
  11.1 17.9 %copy-start.3 = (f32[24,768]{1,0:T(8,128)S(1)}, f32[24,768]{1,0:T(8,128)}, u32[]{:S(2)}) copy-start(f32[24,768]{1,0:T(8,128)} %constant.57.clone) | copy-start | bytes 221188
  11.1 17.9 %copy-start.4 = (f32[24,768]{1,0:T(8,128)S(1)}, f32[24,768]{1,0:T(8,128)}, u32[]{:S(2)}) copy-start(f32[24,768]{1,0:T(8,128)} %constant.58.clone) | copy-start | bytes 221188
  11.1 78.2 %all-to-all-start = ((f32[8,768,96]{2,0,1:T(8,128)}), f32[8,768,96]{2,0,1:T(8,128)}, u32[]{:S(2)}, u32[]{:S(2)}) async-start(f32[8,768,96]{2,0,1:T(8,128)} %copy.21), calls=%async_computation | async-start | bytes 6291456 | tf_op jit(solution)/shard_map/all_to_all | solution.py:194
  28.3 66.4 %copy-start.5 = (f32[3,32]{1,0:T(4,128)}, f32[3,32]{1,0:T(4,128)S(1)}, u32[]{:S(2)}) copy-start(f32[3,32]{1,0:T(4,128)S(1)} %pad_maximum_fusion.coef) | copy-start | bytes 1156
  112.9 13.0 %all-to-all-start.1 = ((f32[2,96,768]{2,0,1:T(2,128)}), f32[2,96,768]{2,0,1:T(2,128)S(1)}, u32[]{:S(2)}, u32[]{:S(2)}) async-start(f32[2,96,768]{2,0,1:T(2,128)} %copy.24), calls=%async_computation.1 | async-start | bytes 1179648 | tf_op jit(solution)/shard_map/all_to_all | solution.py:205
where the time goes:
time: 249 us; the launch traced here: 248 us
  blocking collectives  94.1 us (38%)
  waiting for transfers between devices  66.4 us (27%)
  local copies, waits for them, and re-layouts  33 us (13%)
  matrix products  24.9 us (10%)
  Pallas kernels  12.9 us (5%)
  starting transfers between devices  11.1 us (4%)
  other arithmetic  5.18 us (2%)
    all_to_all x1, blocking collectives, on_device(): lax.all_to_all(along_y, 'pa', split_axis=2, concat_axis=1, tiled=True)  74.4 us
    all_to_all x1, waiting for transfers between devices, on_device(): lax.all_to_all(along_x, 'pa', split_axis=1, concat_axis=2, tiled=True)  58.5 us
    all_to_all x1, blocking collectives, on_device(): sides = lax.all_to_all(sides, 'gz', split_axis=0, concat_axis=1, tiled=True)  13 us
    pallas_call x3, Pallas kernels, solve_call(): pl.pallas_call(kernel, grid=(rows // block,), in_specs=[pl.BlockSpec(memo...  12.9 us
    all_to_all x2, local copies, waits for them, and re-layouts, on_device(): lax.all_to_all(along_x, 'pa', split_axis=1, concat_axis=2, tiled=True)  9.79 us
    all_to_all x2, local copies, waits for them, and re-layouts, on_device(): lax.all_to_all(along_y, 'pa', split_axis=2, concat_axis=1, tiled=True)  7.85 us
    all_to_all x1, waiting for transfers between devices, on_device(): ends = lax.all_to_all(ends, 'gz', split_axis=1, concat_axis=0, tiled=True)  7.85 us
    all_to_all x1, starting transfers between devices, on_device(): lax.all_to_all(along_x, 'pa', split_axis=1, concat_axis=2, tiled=True)  7.43 us
  transfers between devices with their start and end apart: 2, of which 2 were waited for; matrix products, arithmetic and copies ran while one was open for 3% of the time, Pallas kernels for 0%

commit v1 on v0

--- a/solution.py
+++ b/solution.py
@@ -1,3 +1,5 @@
+import functools
+
 import jax
 import jax.numpy as jnp
 import numpy as np
@@ -215,9 +217,436 @@
     )
 
 
+MESH = pl.DeviceIdType.MESH
+NT = (((1,), (1,)), ((), ()))
+NN = (((1,), (0,)), ((), ()))
+
+
+def halves(x):
+    hi = x.astype(jnp.bfloat16)
+    return hi, (x - hi.astype(jnp.float32)).astype(jnp.bfloat16)
+
+
+def block_modes(rows, kind):
+    j, l = np.arange(rows), np.arange(rows)[:, None]
+    if kind == 1:
+        scale = np.sqrt(np.where(l == 0, 1.0, 2.0) / rows)
+        angle = np.pi * l / rows
+        vectors = scale * np.cos(angle * (2 * j + 1) / 2)
+    else:
+        angle = (2 * l + 1) * np.pi / (2 * rows + 1)
+        vectors = 2.0 / np.sqrt(2 * rows + 1) * np.sin(angle * (j + 1))
+    return vectors if kind < 2 else vectors[:, ::-1], 4.0 * np.sin(angle[:, 0] / 2) ** 2
+
+
+def stacked(table):
+    hi = table.astype(jnp.bfloat16)
+    lo = (table - np.asarray(hi, np.float64)).astype(jnp.bfloat16)
+    return np.block([[hi, hi], [lo, np.zeros_like(lo)]])
+
+
+def tables(width, height, parts, depth):
+    k, i = np.arange(width)[:, None], np.arange(width)[None, :]
+    cos = np.sqrt(np.where(k == 0, 1.0, 2.0) / width) * np.cos(np.pi * (k * (2 * i + 1) % (4 * width)) / (2 * width))
+    cos_hi = cos.astype(jnp.bfloat16)
+    cos_lo = (cos - np.asarray(cos_hi, np.float64)).astype(jnp.bfloat16)
+    rows = height // parts
+    phi, edge = [], np.zeros((3, rows, 128), np.float32)
+    for kind in range(3):
+        vectors, values = block_modes(rows, kind)
+        phi.append(np.stack([stacked(vectors), stacked(vectors.T)]))
+        edge[kind, :, 0], edge[kind, :, 1], edge[kind, :, 2] = values, vectors[:, 0], vectors[:, -1]
+    lam = (4.0 * np.sin(np.arange(width) * np.pi / (2 * width)) ** 2).astype(np.float32).reshape(-1, 128)
+    groups = lam.shape[0]
+    targets = 2 * parts
+    lam_t = np.zeros((targets, 128 // targets, 128), np.float32)
+    lam_t[:, :, :groups] = lam.T.reshape(targets, 128 // targets, groups)
+    lam = np.pad(lam, ((0, -groups % 8), (0, 0)))
+    l = np.arange(1, height + 1)[None, :]
+    cut = (np.arange(1, parts) * rows)[:, None]
+    sine = lambda j: np.sqrt(2.0 / (height + 1)) * np.sin(np.pi * (l * j % (2 * (height + 1))) / (height + 1))
+    modes = np.concatenate([4.0 * np.sin(np.pi * l / (2 * (height + 1))) ** 2, sine(cut) - sine(cut + 1)])
+    modes = np.pad(modes, ((0, -parts % 8), (0, 0))).astype(np.float32)
+    return np.stack([cos_hi, cos_lo]), np.stack(phi), edge, lam, lam_t, modes
+
+
+def fused_kernel(
+    size, src, width, cos, phi, edge, lam, lam_t, modes, out,
+    sbuf, s16, ctab, ptab, etab, ltab, lttab, mtab, wbuf, cf, bc, xb, rx, fh, inv, vv,
+    cmine, cpeer, amine, apeer, a2mine, a2peer, eb, et, rb, gt, mb, ginv, gv, st, msg, rb2, e2, uo, xo, ov,
+    in_sem, out_sem, w_send, w_recv, d_send, d_recv, c_send, c_recv, a_send, a_recv, a2_send, a2_recv,
+    x_send, x_recv, y_send, y_recv, u_send, u_recv,
+):
+    parts, slab, rows, depth, pairs, part = size
+    targets = 2 * parts
+    zs, wide = depth * slab, 256
+    lanes = pairs * depth
+    p, g = lax.axis_index("pa"), lax.axis_index("gz")
+    h, c = lax.div(g, 2), lax.rem(g, 2)
+    me = 2 * p + h
+    kind = jnp.where(p == 0, 0, jnp.where(p == parts - 1, 2, 1))
+    twin = {"gz": 2 * h + 1 - c}
+    across = {"gz": 2 * (1 - h) + c}
+    at = lambda t: {"pa": lax.div(t, 2), "gz": 2 * lax.rem(t, 2) + c}
+
+    def remote(source, target, send, recv, device):
+        return pltpu.make_async_remote_copy(
+            src_ref=source, dst_ref=target, send_sem=send, recv_sem=recv, device_id=device, device_id_type=MESH
+        )
+
+    loads = [
+        pltpu.make_async_copy(a, b, in_sem.at[n])
+        for n, (a, b) in enumerate(
+            [(src, sbuf), (cos, ctab), (phi.at[kind], ptab), (edge.at[kind], etab), (lam, ltab), (lam_t.at[me], lttab), (modes, mtab)]
+        )
+    ]
+    for load in loads:
+        load.start()
+    for z in range(slab):
+        wbuf[g, z : z + 1, :] = jnp.full((1, 128), width[z], jnp.float32)
+
+    barrier = pltpu.get_barrier_semaphore()
+    pl.semaphore_signal(barrier, inc=1, device_id=twin, device_id_type=MESH)
+    pl.semaphore_signal(barrier, inc=1, device_id={"gz": 2 * (1 - h) + 1 - c}, device_id_type=MESH)
+    for n in range(1, targets):
+        pl.semaphore_signal(barrier, inc=1, device_id=at(lax.rem(me + n, targets)), device_id_type=MESH)
+    pl.semaphore_wait(barrier, targets + 1)
+
+    widths = lambda n, who: remote(wbuf.at[who], wbuf.at[who], w_send.at[n - 1], w_recv.at[who], {"gz": lax.rem(g + n, 4)})
+    for n in range(1, 4):
+        widths(n, g).start()
+
+    loads[0].wait()
+    s16[0], s16[1] = halves(sbuf[...])
+    loads[1].wait()
+    swap = lambda j: remote(xb.at[2 * j + 1 - c], rx.at[j], d_send.at[j], d_recv.at[j], twin)
+
+    def along_x(j, _):
+        k = pl.ds(pl.multiple_of(wide * j, wide), wide)
+        dot = lambda a, b: lax.dot_general(s16[a], ctab[b, k, :], NT, preferred_element_type=jnp.float32)
+        product = dot(0, 0) + dot(1, 0) + dot(0, 1)
+        xb[2 * j] = product[:, :128]
+        xb[2 * j + 1] = product[:, 128:]
+        swap(j).start()
+        return _
+
+    lax.fori_loop(0, pairs, along_x, 0)
+
+    for n in range(1, 4):
+        widths(n, lax.rem(g + n, 4)).wait_recv()
+    total = 4 * slab
+    w = wbuf[...].reshape(total, 128)
+    z = lax.broadcasted_iota(jnp.int32, (total, 128), 0)
+    cf[0] = 2.0 / (w + jnp.where(z == 0, 0.0, pltpu.roll(w, 1, 0)))
+    cf[1] = 2.0 / (w + jnp.where(z == total - 1, 0.0, pltpu.roll(w, total - 1, 0)))
+    cf[2] = w
+    for load in loads[2:]:
+        load.wait()
+    for n in range(3):
+        bc[n] = jnp.broadcast_to(etab[:, n : n + 1], (rows, 128))
+    for n in range(parts):
+        mb[n] = jnp.broadcast_to(mtab[n : n + 1, :], (8, mtab.shape[1]))
+
+    def cell(zz):
+        zc = zz + h * (depth - 1 - 2 * zz)
+        row = pl.ds(depth * h + zc, 1)
+        return zc, cf[h, row, :], cf[1 - h, row, :], cf[2, row, :]
+
+    swap_c = lambda j: remote(cmine.at[j], cpeer.at[j], c_send.at[j], c_recv.at[j], across)
+
+    def factor(j, _):
+        eigen = bc[0] + ltab[pl.ds(2 * j + c, 1), :]
+        ratio = jnp.zeros((rows, 128), jnp.float32)
+        for zz in range(depth):
+            zc, outer, inner, w = cell(zz)
+            inverse = 1.0 / ((outer + inner) + w * eigen - outer * ratio)
+            inv[j, zc] = inverse
+            ratio = inner * inverse
+        cmine[j] = ratio
+        swap_c(j).start()
+        return _
+
+    lax.fori_loop(0, pairs, factor, 0)
+
+    def transform(which, a, b):
+        hi, lo = halves(jnp.concatenate([a, b], axis=1))
+        both = lax.dot_general(
+            ptab[which], jnp.concatenate([hi, lo], axis=0), NN, preferred_element_type=jnp.float32
+        )
+        both = both[:rows] + both[rows:]
+        return both[:, :128], both[:, 128:]
+
+    swap_a = lambda j: remote(amine.at[j], apeer.at[j], a_send.at[j], a_recv.at[j], across)
+
+    def first(j, _):
+        for n in range(2):
+            if n:
+                swap(j).wait_recv()
+            for zl in range(0, slab, 2):
+                a, b = (slice(rows * y, rows * (y + 1)) for y in (zl, zl + 1))
+                block = (rx.at[j] if n else xb.at[2 * j + c])
+                zc = slab * ((1 - c) if n else c) + zl
+                fh[j, zc], fh[j, zc + 1] = transform(0, block[a, :], block[b, :])
+        value = jnp.zeros((rows, 128), jnp.float32)
+        for zz in range(depth):
+            zc, outer, _inner, w = cell(zz)
+            value = (w * fh[j, zc] + outer * value) * inv[j, zc]
+            vv[j, zc] = value
+        amine[j] = value
+        swap_a(j).start()
+        return _
+
+    lax.fori_loop(0, pairs, first, 0)
+
+    ones = lax.broadcasted_iota(jnp.int32, (part, 128), 1)
+    tiles = mtab.shape[1] // 128
+    eigen_k = [
+        jnp.broadcast_to(jnp.sum(jnp.where(ones == 2 * j + c, lttab[...], 0.0), axis=1, keepdims=True), (part, 128))
+        for j in range(pairs)
+    ]
+
+    def cut_factor(z, ratio):
+        row = pl.ds(z, 1)
+        lower, upper, w = cf[0, row, :], cf[1, row, :], cf[2, row, :]
+        after = []
+        for j in range(pairs):
+            for q in range(tiles):
+                col = slice(128 * q, 128 * q + 128)
+                inverse = 1.0 / ((lower + upper) + w * (eigen_k[j] + mb[0, :, col]) - lower * ratio[j * tiles + q])
+                ginv[z, part * j : part * (j + 1), col] = inverse
+                after.append(upper * inverse)
+        return tuple(after)
+
+    zero = jnp.zeros((part, 128), jnp.float32)
+    lax.fori_loop(0, total, cut_factor, (zero,) * (pairs * tiles))
+
+    def middle(j, mine, peer):
+        return (mine[j] + cmine[j] * peer[j]) / (1.0 - cmine[j] * cpeer[j])
+
+    eb[2 * lanes :, :] = jnp.zeros((128 - 2 * lanes, 128), jnp.float32)
+
+    def first_back(j, _):
+        swap_c(j).wait_recv()
+        swap_a(j).wait_recv()
+        x = middle(j, amine, apeer)
+        for zz in reversed(range(depth)):
+            zc, _outer, inner, w = cell(zz)
+            if zz < depth - 1:
+                x = vv[j, zc] + inner * inv[j, zc] * x
+            for n in range(2):
+                eb[pl.ds(lanes * n + depth * j + zc, 1), :] = jnp.sum(bc[1 + n] * x, axis=0, keepdims=True)
+        return _
+
+    lax.fori_loop(0, pairs, first_back, 0)
+
+    et[...] = jnp.transpose(eb[...])
+    piece = lambda t: pl.ds(pl.multiple_of(part * t, part), part)
+    send_x = lambda n, t, who: remote(et.at[piece(t), :], rb.at[who], x_send.at[n - 1], x_recv.at[who], at(t))
+    for n in range(1, targets):
+        send_x(n, lax.rem(me + n, targets), me).start()
+    rb[me] = et[piece(me), :]
+    for n in range(1, targets):
+        t = lax.rem(me + n, targets)
+        send_x(n, t, t).wait_recv()
+    lane = lax.broadcasted_iota(jnp.int32, (part, 128), 1)
+    for i in range(parts - 1):
+        for y in range(2):
+            jump = pltpu.roll(rb[2 * i + y], 128 - lanes, 1) - rb[2 * i + 2 + y]
+            gt[2 * i + y] = jnp.where(lane < lanes, jump, 0.0)
+
+    def cut_forward(y, value):
+        value = list(value)
+        for zc in range(depth):
+            z = depth * y + zc
+            row = pl.ds(z, 1)
+            lower, w = cf[0, row, :], cf[2, row, :]
+            for j in range(pairs):
+                at_lane = slice(depth * j + zc, depth * j + zc + 1)
+                force = [w * jnp.broadcast_to(gt[2 * i + y, :, at_lane], (part, 128)) for i in range(parts - 1)]
+                for q in range(tiles):
+                    col = slice(128 * q, 128 * q + 128)
+                    s = j * tiles + q
+                    rhs = lower * value[s]
+                    for i in range(parts - 1):
+                        rhs = rhs + force[i] * mb[1 + i, :, col]
+                    value[s] = rhs * ginv[z, part * j : part * (j + 1), col]
+                    gv[z, part * j : part * (j + 1), col] = value[s]
+        return tuple(value)
+
+    lax.fori_loop(0, 2, cut_forward, (zero,) * (pairs * tiles))
+
+    def cut_back(n, x):
+        x = list(x)
+        y = 1 - n
+        sums = [zero] * (parts - 1)
+        for zc in reversed(range(depth)):
+            z = depth * y + zc
+            upper = cf[1, pl.ds(z, 1), :]
+            for j in range(pairs):
+                along = [zero] * (parts - 1)
+                for q in range(tiles):
+                    col = slice(128 * q, 128 * q + 128)
+                    s = j * tiles + q
+                    r = slice(part * j, part * (j + 1))
+                    x[s] = gv[z, r, col] + upper * ginv[z, r, col] * x[s]
+                    for i in range(parts - 1):
+                        along[i] = along[i] + mb[1 + i, :, col] * x[s]
+                for i in range(parts - 1):
+                    sums[i] = jnp.where(lane == depth * j + zc, jnp.sum(along[i], axis=1, keepdims=True), sums[i])
+        for i in range(parts - 1):
+            st[2 * i + y] = gt[2 * i + y] - sums[i]
+        return tuple(x)
+
+    lax.fori_loop(0, 2, cut_back, (zero,) * (pairs * tiles))
+
+    for q in range(parts):
+        for y in range(2):
+            left = st[2 * (q - 1) + y] if q else zero
+            right = pltpu.roll(st[2 * q + y], lanes, 1) if q < parts - 1 else zero
+            msg[2 * q + y] = left + right
+    send_y = lambda n, t, who: remote(msg.at[t], rb2.at[who], y_send.at[n - 1], y_recv.at[who], at(t))
+    for n in range(1, targets):
+        send_y(n, lax.rem(me + n, targets), me).start()
+    rb2[me] = msg[me]
+    for n in range(1, targets):
+        t = lax.rem(me + n, targets)
+        send_y(n, t, t).wait_recv()
+    e2[...] = jnp.transpose(rb2[...].reshape(128, 128))
+
+    swap_a2 = lambda j: remote(a2mine.at[j], a2peer.at[j], a2_send.at[j], a2_recv.at[j], across)
+
+    def second(j, _):
+        value = jnp.zeros((rows, 128), jnp.float32)
+        for zz in range(depth):
+            zc, outer, _inner, w = cell(zz)
+            left = e2[pl.ds(depth * j + zc, 1), :]
+            right = e2[pl.ds(lanes + depth * j + zc, 1), :]
+            force = fh[j, zc] + bc[1] * left - bc[2] * right
+            value = (w * force + outer * value) * inv[j, zc]
+            vv[j, zc] = value
+        a2mine[j] = value
+        swap_a2(j).start()
+        return _
+
+    lax.fori_loop(0, pairs, second, 0)
+
+    swap_u = lambda j, who: remote(uo.at[j], xo.at[2 * j + who], u_send.at[j], u_recv.at[j], twin)
+
+    def second_back(j, _):
+        swap_a2(j).wait_recv()
+        x = middle(j, a2mine, a2peer)
+        for zz in reversed(range(depth)):
+            zc, _outer, inner, w = cell(zz)
+            if zz < depth - 1:
+                x = vv[j, zc] + inner * inv[j, zc] * x
+            fh[j, zc] = x
+        for n in range(2):
+            for zl in range(0, slab, 2):
+                a, b = (slice(rows * y, rows * (y + 1)) for y in (zl, zl + 1))
+                zc = slab * (c if n else (1 - c)) + zl
+                block = xo.at[2 * j + c] if n else uo.at[j]
+                block[a, :], block[b, :] = transform(1, fh[j, zc], fh[j, zc + 1])
+            if n == 0:
+                swap_u(j, c).start()
+        return _
+
+    lax.fori_loop(0, pairs, second_back, 0)
+
+    def split(j, who):
+        k = 2 * j + who
+        cols = pl.ds(pl.multiple_of(128 * k, 128), 128)
+        s16[0, :, cols], s16[1, :, cols] = halves(xo[k])
+
+    for j in range(pairs):
+        split(j, c)
+    for j in range(pairs):
+        swap_u(j, 1 - c).wait_recv()
+        split(j, 1 - c)
+
+    put = lambda j: pltpu.make_async_copy(
+        ov.at[j], out.at[:, pl.ds(pl.multiple_of(wide * j, wide), wide)], out_sem.at[j]
+    )
+
+    def back_x(j, _):
+        i = pl.ds(pl.multiple_of(wide * j, wide), wide)
+        dot = lambda a, b: lax.dot_general(s16[a], ctab[b, :, i], NN, preferred_element_type=jnp.float32)
+        ov[j] = dot(0, 0) + dot(1, 0) + dot(0, 1)
+        put(j).start()
+        return _
+
+    lax.fori_loop(0, pairs, back_x, 0)
+
+    for n in range(1, 4):
+        widths(n, g).wait_send()
+    for n in range(1, targets):
+        send_x(n, lax.rem(me + n, targets), me).wait_send()
+        send_y(n, lax.rem(me + n, targets), me).wait_send()
+    for j in range(pairs):
+        swap(j).wait_send()
+        swap_c(j).wait_send()
+        swap_a(j).wait_send()
+        swap_a2(j).wait_send()
+        swap_u(j, c).wait_send()
+        put(j).wait()
+
+
+def fused(source, cell_width):
+    slab, rows, nx = source.shape
+    parts = lax.axis_size("pa")
+    pairs, depth, targets = nx // 256, 2 * slab, 2 * parts
+    part = 128 // targets
+    ny = rows * parts
+    consts = tables(nx, ny, parts, depth)
+    f32, b16, V = jnp.float32, jnp.bfloat16, pltpu.VMEM
+    tall = slab * rows
+    lines = (pairs, depth, rows, 128)
+    plane = (pairs, rows, 128)
+    cuts = (2 * slab * 2, part * pairs, ny)
+    sem = lambda n: pltpu.SemaphoreType.DMA((n,))
+    scratch = [
+        V((tall, nx), f32), V((2, tall, nx), b16), V((2, nx, nx), b16), V((2, 2 * rows, 2 * rows), b16), V((rows, 128), f32),
+        V(consts[3].shape, f32), V((part, 128), f32), V(consts[5].shape, f32), V((4, slab, 128), f32),
+        V((3, 4 * slab, 128), f32), V((3, rows, 128), f32),
+        V((2 * pairs, tall, 128), f32), V((pairs, tall, 128), f32), V(lines, f32), V(lines, f32), V(lines, f32),
+        V(plane, f32), V(plane, f32), V(plane, f32), V(plane, f32), V(plane, f32), V(plane, f32),
+        V((128, 128), f32), V((128, 128), f32), V((targets, part, 128), f32), V((targets, part, 128), f32),
+        V((parts, 8, ny), f32), V(cuts, f32), V(cuts, f32),
+        V((targets, part, 128), f32), V((targets, part, 128), f32), V((targets, part, 128), f32), V((128, 128), f32),
+        V((pairs, tall, 128), f32), V((2 * pairs, tall, 128), f32), V((pairs, tall, 256), f32),
+        sem(7), sem(pairs), sem(3), sem(4), sem(pairs), sem(pairs), sem(pairs), sem(pairs), sem(pairs), sem(pairs),
+        sem(pairs), sem(pairs), sem(targets), sem(targets), sem(targets), sem(targets), sem(pairs), sem(pairs),
+    ]
+    hbm = pl.BlockSpec(memory_space=pltpu.HBM)
+    out = pl.pallas_call(
+        functools.partial(fused_kernel, (parts, slab, rows, depth, pairs, part)),
+        out_shape=jax.ShapeDtypeStruct((tall, nx), f32),
+        in_specs=[hbm, pl.BlockSpec(memory_space=pltpu.SMEM)] + [hbm] * 6,
+        out_specs=hbm,
+        scratch_shapes=scratch,
+        compiler_params=pltpu.CompilerParams(
+            collective_id=0, has_side_effects=True, vmem_limit_bytes=60 * 1024 * 1024
+        ),
+    )(source.reshape(tall, nx), cell_width, *(jnp.asarray(t) for t in consts))
+    return out.reshape(slab, rows, nx)
+
+
+def fits(source, parts, blocks):
+    slab, rows, nx = source.shape
+    return (
+        blocks == 4 and parts == 8 and nx % 256 == 0 and slab == 8 and rows % 16 == 0
+        and (rows * parts) % 128 == 0 and 2 * (nx // 256) * 2 * slab <= 128
+    )
+
+
+def per_device(source, cell_width):
+    if fits(source, lax.axis_size("pa"), lax.axis_size("gz")):
+        return fused(source, cell_width)
+    return on_device(source, cell_width)
+
+
 def solution(mesh):
     in_specs = (P("gz", "pa", None), P("gz"))
     out_specs = P("gz", "pa", None)
     return jax.shard_map(
-        on_device, mesh=mesh, in_specs=in_specs, out_specs=out_specs, check_vma=False
+        per_device, mesh=mesh, in_specs=in_specs, out_specs=out_specs, check_vma=False
     )

time: 249 us -> 47.4 us (0.19)
  blocking collectives: 94.1 us -> 0 us
  waiting for transfers between devices: 66.4 us -> 0 us
  Pallas kernels: 12.9 us -> 43.4 us
  local copies, waits for them, and re-layouts: 33 us -> 3.22 us
  matrix products: 24.9 us -> 0 us
  starting transfers between devices: 11.1 us -> 0 us
  other arithmetic: 5.18 us -> 0 us
    all_to_all x2 -> x0, blocking collectives: 87.4 us -> none  [the longest x1 74.4 us: on_device(): lax.all_to_all(along_y, 'pa', split_axis=2, concat_axis=1, tiled=True)]
    all_to_all x2 -> x0, waiting for transfers between devices: 66.4 us -> none  [the longest x1 58.5 us: on_device(): lax.all_to_all(along_x, 'pa', split_axis=1, concat_axis=2, tiled=True)]
    pallas_call x3 -> x1, Pallas kernels: 12.9 us -> 43.4 us  [fused(): pl.pallas_call(functools.partial(fused_kernel, (parts, slab, rows, depth,...]
    dot_general x4 -> x0, matrix products: 24.9 us -> none  [the longest x1 6.87 us: on_device(): along_y = jnp.einsum('zkl,lj->zkj', solved, sin_table, precision=HIGH)]
    all_to_all x6 -> x0, local copies, waits for them, and re-layouts: 19.4 us -> none  [the longest x2 9.79 us: on_device(): lax.all_to_all(along_x, 'pa', split_axis=1, concat_axis=2, tiled=True)]
    all_to_all x2 -> x0, starting transfers between devices: 11.1 us -> none  [the longest x1 7.43 us: on_device(): lax.all_to_all(along_x, 'pa', split_axis=1, concat_axis=2, tiled=True)]
    unnamed x1 -> x0, blocking collectives: 6.7 us -> none
    mul x3 -> x0, other arithmetic: 5.07 us -> none  [the longest x2 3.26 us: cosine_table(): return weights * summed_angles(width, a, b, False)]
  transfers between devices with their start and end apart: 2 -> 0, of which waited for: 2 -> 0; matrix products, arithmetic and copies ran while one was open for 3% -> 0% of each run, Pallas kernels for 0% -> 0%
where the time goes in v1:
time: 47.4 us; the launch traced here: 46.7 us
  Pallas kernels  43.4 us (92%)
  local copies, waits for them, and re-layouts  3.22 us (7%)
    pallas_call x1, Pallas kernels, fused(): pl.pallas_call(functools.partial(fused_kernel, (parts, slab, rows, depth,...  43.4 us
    unnamed x1, local copies, waits for them, and re-layouts  3.22 us

profile of v1, /device:TPU:0, one launch (start us, length us, event | category | flops | bytes accessed | tf_op | source)
XLA Modules:
  0.0 46.7 jit_solution(4474164218958451387)
XLA Ops:
  0.0 43.4 %shard_map.82 = f32[768,768]{1,0:T(8,128)} custom-call(f32[768,768]{1,0:T(8,128)} %bitcast.3, f32[8]{0:T(128)} %width.1, bf16[2,768,768]{2,1,0:T(8,128)(2,1)} %constant.12.clone.cos, bf16[3,2,192,192]{3,2,1,0:T(8,128)(2,1)} %constant.13.clone.phi, f32[3,96,128]{2,1,0:T(8,128)} %constant.14.clone.edge, f32[8,128]{1,0:T(8,128)} %constant.15.clone.lam, ...), custom_call_target="tpu_custom_call" | custom-call | tf_op jit(solution)/shard_map/pallas_call | solution.py:620
  43.4 3.2 %copy.10 = f32[8,96,768]{2,1,0:T(8,128)} copy(f32[8,96,768]{2,1,0:T(8,128)} %bitcast.2) | data formatting | bytes 4718592

commit v2 on v0

--- a/solution.py
+++ b/solution.py
@@ -1,3 +1,5 @@
+import functools
+
 import jax
 import jax.numpy as jnp
 import numpy as np
@@ -215,9 +217,440 @@
     )
 
 
+MESH = pl.DeviceIdType.MESH
+NT = (((1,), (1,)), ((), ()))
+NN = (((1,), (0,)), ((), ()))
+SOURCE_PIECES = 4
+
+
+def halves(x):
+    hi = x.astype(jnp.bfloat16)
+    return hi, (x - hi.astype(jnp.float32)).astype(jnp.bfloat16)
+
+
+def block_modes(rows, kind):
+    j, l = np.arange(rows), np.arange(rows)[:, None]
+    if kind == 1:
+        scale = np.sqrt(np.where(l == 0, 1.0, 2.0) / rows)
+        angle = np.pi * l / rows
+        vectors = scale * np.cos(angle * (2 * j + 1) / 2)
+    else:
+        angle = (2 * l + 1) * np.pi / (2 * rows + 1)
+        vectors = 2.0 / np.sqrt(2 * rows + 1) * np.sin(angle * (j + 1))
+    return vectors if kind < 2 else vectors[:, ::-1], 4.0 * np.sin(angle[:, 0] / 2) ** 2
+
+
+def stacked(table):
+    hi = table.astype(jnp.bfloat16)
+    lo = (table - np.asarray(hi, np.float64)).astype(jnp.bfloat16)
+    return np.block([[hi, hi], [lo, np.zeros_like(lo)]])
+
+
+def tables(width, height, parts, depth):
+    k, i = np.arange(width)[:, None], np.arange(width)[None, :]
+    cos = np.sqrt(np.where(k == 0, 1.0, 2.0) / width) * np.cos(np.pi * (k * (2 * i + 1) % (4 * width)) / (2 * width))
+    cos_hi = cos.astype(jnp.bfloat16)
+    cos_lo = (cos - np.asarray(cos_hi, np.float64)).astype(jnp.bfloat16)
+    rows = height // parts
+    phi, edge = [], np.zeros((3, rows, 128), np.float32)
+    for kind in range(3):
+        vectors, values = block_modes(rows, kind)
+        phi.append(np.stack([stacked(vectors), stacked(vectors.T)]))
+        edge[kind, :, 0], edge[kind, :, 1], edge[kind, :, 2] = values, vectors[:, 0], vectors[:, -1]
+    lam = (4.0 * np.sin(np.arange(width) * np.pi / (2 * width)) ** 2).astype(np.float32).reshape(-1, 128)
+    groups = lam.shape[0]
+    targets = 2 * parts
+    lam_t = np.zeros((targets, 128 // targets, 128), np.float32)
+    lam_t[:, :, :groups] = lam.T.reshape(targets, 128 // targets, groups)
+    lam = np.pad(lam, ((0, -groups % 8), (0, 0)))
+    l = np.arange(1, height + 1)
+    l = np.concatenate([l[::2], l[1::2]])[None, :]
+    cut = (np.arange(1, parts // 2 + 1) * rows)[:, None]
+    sine = lambda j: np.sqrt(2.0 / (height + 1)) * np.sin(np.pi * (l * j % (2 * (height + 1))) / (height + 1))
+    modes = np.concatenate([4.0 * np.sin(np.pi * l / (2 * (height + 1))) ** 2, sine(cut) - sine(cut + 1)])
+    modes = np.pad(modes, ((0, -len(modes) % 8), (0, 0))).astype(np.float32)
+    return np.stack([cos_hi, cos_lo]), np.stack(phi), edge, lam, lam_t, modes
+
+
+def fused_kernel(
+    size, src, width, cos, phi, edge, lam, lam_t, modes, out,
+    sbuf, s16, ctab, ptab, etab, ltab, lttab, mtab, wbuf, cf, bc, xb, rx, fh, inv, vv,
+    inv2, cmine, cpeer, join, amine, apeer, eb, et, rb, gt, mb, ginv, gv, msg, rb2, e2, uo, xo,
+    in_sem, src_sem, cos_sem, w_send, w_recv, d_send, d_recv, a_send, a_recv,
+    x_send, x_recv, y_send, y_recv, u_send, u_recv,
+):
+    parts, slab, rows, depth, pairs, part = size
+    targets = 2 * parts
+    wide, lanes = 256, 4 * depth
+    tall = slab * rows
+    cuts, half = parts - 1, (parts - 1) // 2
+    p, g = lax.axis_index("pa"), lax.axis_index("gz")
+    h, c = lax.div(g, 2), lax.rem(g, 2)
+    me = 2 * p + h
+    kind = jnp.where(p == 0, 0, jnp.where(p == parts - 1, 2, 1))
+    twin = {"gz": 2 * h + 1 - c}
+    across = {"gz": 2 * (1 - h) + c}
+    at = lambda t: {"pa": lax.div(t, 2), "gz": 2 * lax.rem(t, 2) + c}
+
+    def remote(source, target, send, recv, device):
+        return pltpu.make_async_remote_copy(
+            src_ref=source, dst_ref=target, send_sem=send, recv_sem=recv, device_id=device, device_id_type=MESH
+        )
+
+    quarter = tall // SOURCE_PIECES
+    load_src = lambda n: pltpu.make_async_copy(
+        src.at[quarter * n : quarter * (n + 1), :], sbuf.at[quarter * n : quarter * (n + 1), :], src_sem.at[n]
+    )
+    group = lambda j: pl.ds(pl.multiple_of(wide * j, wide), wide)
+    load_cos = lambda j: pltpu.make_async_copy(cos.at[:, group(j), :], ctab.at[:, group(j), :], cos_sem.at[j])
+    loads = [
+        pltpu.make_async_copy(a, b, in_sem.at[n])
+        for n, (a, b) in enumerate(
+            [(phi.at[kind], ptab), (edge.at[kind], etab), (lam, ltab), (lam_t.at[me], lttab), (modes, mtab)]
+        )
+    ]
+    for n in range(SOURCE_PIECES):
+        load_src(n).start()
+    load_cos(0).start()
+    for load in loads:
+        load.start()
+    for j in range(1, pairs):
+        load_cos(j).start()
+    for z in range(slab):
+        wbuf[g, z : z + 1, :] = jnp.full((1, 128), width[z], jnp.float32)
+
+    barrier = pltpu.get_barrier_semaphore()
+    pl.semaphore_signal(barrier, inc=1, device_id=twin, device_id_type=MESH)
+    pl.semaphore_signal(barrier, inc=1, device_id={"gz": 2 * (1 - h) + 1 - c}, device_id_type=MESH)
+    for n in range(1, targets):
+        pl.semaphore_signal(barrier, inc=1, device_id=at(lax.rem(me + n, targets)), device_id_type=MESH)
+    pl.semaphore_wait(barrier, targets + 1)
+
+    widths = lambda n, who: remote(wbuf.at[who], wbuf.at[who], w_send.at[n - 1], w_recv.at[who], {"gz": lax.rem(g + n, 4)})
+    for n in range(1, 4):
+        widths(n, g).start()
+
+    for n in range(SOURCE_PIECES):
+        load_src(n).wait()
+        r = slice(quarter * n, quarter * (n + 1))
+        s16[0, r, :], s16[1, r, :] = halves(sbuf[r, :])
+
+    swap = lambda j: remote(xb.at[2 * j + 1 - c], rx.at[j], d_send.at[j], d_recv.at[j], twin)
+    swap_a = lambda j: remote(amine.at[j], apeer.at[j], a_send.at[j], a_recv.at[j], across)
+    swap_u = lambda j, who: remote(uo.at[j], xo.at[2 * j + who], u_send.at[j], u_recv.at[j], twin)
+    piece = lambda t: pl.ds(pl.multiple_of(part * t, part), part)
+    send_x = lambda j, n, t, who: remote(
+        et.at[j, piece(t), :], rb.at[j, who], x_send.at[j, n - 1], x_recv.at[j, who], at(t)
+    )
+    send_y = lambda j, n, t, who: remote(msg.at[j, lax.div(t, 2)], rb2.at[j, who], y_send.at[j, n - 1], y_recv.at[j, who], at(t))
+    peer_of = lambda n: lax.rem(me + n, targets)
+    zero = jnp.zeros((part, 128), jnp.float32)
+    lane = lax.broadcasted_iota(jnp.int32, (part, 128), 1)
+    total = 4 * slab
+    tiles = mtab.shape[1] // 128
+
+    def cell(zz, side):
+        zc = zz + side * (depth - 1 - 2 * zz)
+        z = depth * side + zc
+        row = pl.ds(z, 1)
+        return zc, z, cf[side, row, :], cf[1 - side, row, :], cf[2, row, :]
+
+    def along_x(j):
+        load_cos(j).wait()
+        dot = lambda a, b: lax.dot_general(s16[a], ctab[b, group(j), :], NT, preferred_element_type=jnp.float32)
+        product = dot(0, 0) + dot(1, 0) + dot(0, 1)
+        xb[2 * j] = product[:, :128]
+        xb[2 * j + 1] = product[:, 128:]
+        swap(j).start()
+
+    def coefficients():
+        for n in range(1, 4):
+            widths(n, lax.rem(g + n, 4)).wait_recv()
+        w = wbuf[...].reshape(total, 128)
+        z = lax.broadcasted_iota(jnp.int32, (total, 128), 0)
+        cf[0] = 2.0 / (w + jnp.where(z == 0, 0.0, pltpu.roll(w, 1, 0)))
+        cf[1] = 2.0 / (w + jnp.where(z == total - 1, 0.0, pltpu.roll(w, total - 1, 0)))
+        cf[2] = w
+        for load in loads:
+            load.wait()
+        for n in range(3):
+            bc[n] = jnp.broadcast_to(etab[:, n : n + 1], (rows, 128))
+        for n in range(half + 2):
+            mb[n] = jnp.broadcast_to(mtab[n : n + 1, :], (8, mtab.shape[1]))
+        eb[lanes:, :] = jnp.zeros((128 - lanes, 128), jnp.float32)
+
+    def transform(which, a, b):
+        hi, lo = halves(jnp.concatenate([a, b], axis=1))
+        both = lax.dot_general(
+            ptab[which], jnp.concatenate([hi, lo], axis=0), NN, preferred_element_type=jnp.float32
+        )
+        both = both[:rows] + both[rows:]
+        return both[:, :128], both[:, 128:]
+
+    def first(j):
+        eigen = bc[0] + ltab[pl.ds(2 * j + c, 1), :]
+        ratios = [jnp.zeros((rows, 128), jnp.float32)] * 2
+        for zz in range(depth):
+            for n, (side, keep) in enumerate([(h, inv), (1 - h, inv2)]):
+                zc, _z, outer, inner, w = cell(zz, side)
+                inverse = 1.0 / ((outer + inner) + w * eigen - outer * ratios[n])
+                keep[j, zc] = inverse
+                ratios[n] = inner * inverse
+        cmine[j], cpeer[j] = ratios
+        join[j] = 1.0 / (1.0 - ratios[0] * ratios[1])
+        for n in range(2):
+            if n:
+                swap(j).wait_recv()
+            for zl in range(0, slab, 2):
+                a, b = (slice(rows * y, rows * (y + 1)) for y in (zl, zl + 1))
+                block = rx.at[j] if n else xb.at[2 * j + c]
+                zc = slab * ((1 - c) if n else c) + zl
+                fh[j, zc], fh[j, zc + 1] = transform(0, block[a, :], block[b, :])
+        value = jnp.zeros((rows, 128), jnp.float32)
+        for zz in range(depth):
+            zc, _z, outer, _inner, w = cell(zz, h)
+            value = (w * fh[j, zc] + outer * value) * inv[j, zc]
+            vv[j, zc] = value
+        amine[j] = value
+        swap_a(j).start()
+
+    def first_back(j):
+        x = amine[j] * join[j]
+        y = cpeer[j] * x
+        for zz in reversed(range(depth)):
+            zc, z, _outer, inner, _w = cell(zz, h)
+            yc, yz, _outer, across_in, _w = cell(zz, 1 - h)
+            if zz < depth - 1:
+                x = vv[j, zc] + inner * inv[j, zc] * x
+                y = across_in * inv2[j, yc] * y
+            for n in range(2):
+                eb[pl.ds(2 * depth * n + z, 1), :] = jnp.sum(bc[1 + n] * x, axis=0, keepdims=True)
+                eb[pl.ds(2 * depth * n + yz, 1), :] = jnp.sum(bc[1 + n] * y, axis=0, keepdims=True)
+        et[j] = jnp.transpose(eb[...])[:, :lanes]
+        for n in range(1, targets):
+            send_x(j, n, peer_of(n), me).start()
+        rb[j, me] = et[j, piece(me), :]
+
+    def cut_factors():
+        eigen_k = [
+            jnp.broadcast_to(jnp.sum(jnp.where(lane == 2 * j + c, lttab[...], 0.0), axis=1, keepdims=True), (part, 128))
+            for j in range(pairs)
+        ]
+
+        def cut_factor(z, ratio):
+            row = pl.ds(z, 1)
+            lower, upper, w = cf[0, row, :], cf[1, row, :], cf[2, row, :]
+            after = []
+            for j in range(pairs):
+                for q in range(tiles):
+                    col = slice(128 * q, 128 * q + 128)
+                    inverse = 1.0 / ((lower + upper) + w * (eigen_k[j] + mb[0, :, col]) - lower * ratio[j * tiles + q])
+                    ginv[j, z, :, col] = inverse
+                    after.append(upper * inverse)
+            return tuple(after)
+
+        lax.fori_loop(0, total, cut_factor, (zero,) * (pairs * tiles))
+
+    def head(step, carry):
+        @pl.when(step < pairs)
+        def _():
+            along_x(step)
+
+        @pl.when(step == 1)
+        def _():
+            coefficients()
+
+        @pl.when(step >= 1)
+        def _():
+            first(step - 1)
+            first_back(step - 1)
+
+        return carry
+
+    lax.fori_loop(0, pairs + 1, head, 0)
+    cut_factors()
+
+    terms = lambda q: range(half) if q < tiles // 2 else range(half, cuts)
+    mode = lambda m: 1 + (m if m < half else m - half)
+
+    def cut(j, carry):
+        for n in range(1, targets):
+            t = peer_of(n)
+            send_x(j, n, t, t).wait_recv()
+        edge = [rb[j, 2 * i] + rb[j, 2 * i + 1] for i in range(parts)]
+        jump = [edge[i][:, 2 * depth :] - edge[i + 1][:, : 2 * depth] for i in range(cuts)]
+        mixed = [jump[i] - jump[cuts - 1 - i] for i in range(half)]
+        mixed += [jump[i] + jump[cuts - 1 - i] for i in range(half)] + [jump[half]]
+        for i in range(cuts):
+            gt[i, :, : 2 * depth] = jump[i]
+        value = [zero] * tiles
+        for z in range(total):
+            lower, w = cf[0, z : z + 1, :], cf[2, z : z + 1, :]
+            force = [w * jnp.broadcast_to(m[:, z : z + 1], (part, 128)) for m in mixed]
+            for q in range(tiles):
+                col = slice(128 * q, 128 * q + 128)
+                rhs = lower * value[q]
+                for m in terms(q):
+                    rhs = rhs + force[m] * mb[mode(m), :, col]
+                value[q] = rhs * ginv[j, z, :, col]
+                gv[z, :, col] = value[q]
+
+        x = [zero] * tiles
+        sums = [zero] * cuts
+        for z in reversed(range(total)):
+            upper = cf[1, z : z + 1, :]
+            along = [zero] * cuts
+            for q in range(tiles):
+                col = slice(128 * q, 128 * q + 128)
+                x[q] = gv[z, :, col] + upper * ginv[j, z, :, col] * x[q]
+                for m in terms(q):
+                    along[m] = along[m] + mb[mode(m), :, col] * x[q]
+            for m in range(cuts):
+                sums[m] = jnp.where(lane == z, jnp.sum(along[m], axis=1, keepdims=True), sums[m])
+        true = [zero] * cuts
+        for i in range(half):
+            true[i] = gt[i] - (sums[half + i] + sums[i])
+            true[cuts - 1 - i] = gt[cuts - 1 - i] - (sums[half + i] - sums[i])
+        true[half] = gt[half] - sums[cuts - 1]
+        for q in range(parts):
+            left = true[q - 1] if q else zero
+            right = pltpu.roll(true[q], 2 * depth, 1) if q < parts - 1 else zero
+            msg[j, q] = (left + right)[:, :lanes]
+        for n in range(1, targets):
+            send_y(j, n, peer_of(n), me).start()
+        rb2[j, me] = msg[j, p]
+        return carry
+
+    gt[...] = jnp.zeros(gt.shape, jnp.float32)
+    lax.fori_loop(0, pairs, cut, 0)
+
+    def second(j):
+        for n in range(1, targets):
+            t = peer_of(n)
+            send_y(j, n, t, t).wait_recv()
+        e2[...] = jnp.transpose(rb2[j].reshape(128, lanes))
+        value = jnp.zeros((rows, 128), jnp.float32)
+        other = value
+        for zz in range(depth):
+            zc, z, outer, _inner, w = cell(zz, h)
+            left, right = e2[pl.ds(z, 1), :], e2[pl.ds(2 * depth + z, 1), :]
+            force = fh[j, zc] + bc[1] * left - bc[2] * right
+            value = (w * force + outer * value) * inv[j, zc]
+            vv[j, zc] = value
+            zc, z, outer, _inner, w = cell(zz, 1 - h)
+            left, right = e2[pl.ds(z, 1), :], e2[pl.ds(2 * depth + z, 1), :]
+            other = (w * (bc[1] * left - bc[2] * right) + outer * other) * inv2[j, zc]
+        swap_a(j).wait_recv()
+        x = (value + cmine[j] * (apeer[j] + other)) * join[j]
+        for zz in reversed(range(depth)):
+            zc, _z, _outer, inner, _w = cell(zz, h)
+            if zz < depth - 1:
+                x = vv[j, zc] + inner * inv[j, zc] * x
+            fh[j, zc] = x
+        for n in range(2):
+            for zl in range(0, slab, 2):
+                a, b = (slice(rows * y, rows * (y + 1)) for y in (zl, zl + 1))
+                zc = slab * (c if n else (1 - c)) + zl
+                block = xo.at[2 * j + c] if n else uo.at[j]
+                block[a, :], block[b, :] = transform(1, fh[j, zc], fh[j, zc + 1])
+            if n == 0:
+                swap_u(j, c).start()
+
+    def back_x(j):
+        swap_u(j, 1 - c).wait_recv()
+        for n in range(2):
+            s16[0, :, 128 * n : 128 * n + 128], s16[1, :, 128 * n : 128 * n + 128] = halves(xo[2 * j + n])
+        for n in range(pairs):
+            i = slice(wide * n, wide * (n + 1))
+            dot = lambda a, b: lax.dot_general(
+                s16[a, :, :wide], ctab[b, group(j), i], NN, preferred_element_type=jnp.float32
+            )
+            out[:, i] = out[:, i] + (dot(0, 0) + dot(1, 0) + dot(0, 1))
+
+    def tail(step, carry):
+        @pl.when(step < pairs)
+        def _():
+            second(step)
+
+        @pl.when(step >= 1)
+        def _():
+            back_x(step - 1)
+
+        return carry
+
+    out[...] = jnp.zeros(out.shape, jnp.float32)
+    lax.fori_loop(0, pairs + 1, tail, 0)
+
+    for n in range(1, 4):
+        widths(n, g).wait_send()
+    for j in range(pairs):
+        for n in range(1, targets):
+            send_x(j, n, peer_of(n), me).wait_send()
+            send_y(j, n, peer_of(n), me).wait_send()
+        swap(j).wait_send()
+        swap_a(j).wait_send()
+        swap_u(j, c).wait_send()
+
+
+def fused(source, cell_width):
+    slab, rows, nx = source.shape
+    parts = lax.axis_size("pa")
+    pairs, depth, targets = nx // 256, 2 * slab, 2 * parts
+    part = 128 // targets
+    ny = rows * parts
+    consts = tables(nx, ny, parts, depth)
+    f32, b16, V = jnp.float32, jnp.bfloat16, pltpu.VMEM
+    tall = slab * rows
+    lines = (pairs, depth, rows, 128)
+    plane = (pairs, rows, 128)
+    sem = lambda *n: pltpu.SemaphoreType.DMA(n)
+    lanes = 4 * depth
+    small = (pairs, targets, part, lanes)
+    scratch = [
+        V((tall, nx), f32), V((2, tall, nx), b16), V((2, nx, nx), b16), V((2, 2 * rows, 2 * rows), b16), V((rows, 128), f32),
+        V(consts[3].shape, f32), V((part, 128), f32), V(consts[5].shape, f32), V((4, slab, 128), f32),
+        V((3, 4 * slab, 128), f32), V((3, rows, 128), f32),
+        V((2 * pairs, tall, 128), f32), V((pairs, tall, 128), f32), V(lines, f32), V(lines, f32), V(lines, f32),
+        V(lines, f32), V(plane, f32), V(plane, f32), V(plane, f32), V(plane, f32), V(plane, f32),
+        V((128, 128), f32), V((pairs, 128, lanes), f32), V(small, f32), V((parts, part, 128), f32),
+        V((parts // 2 + 1, 8, ny), f32), V((pairs, 2 * depth, part, ny), f32), V((2 * depth, part, ny), f32),
+        V((pairs, parts, part, lanes), f32), V(small, f32), V((lanes, 128), f32),
+        V((pairs, tall, 128), f32), V((2 * pairs, tall, 128), f32),
+        sem(5), sem(SOURCE_PIECES), sem(pairs), sem(3), sem(4), sem(pairs), sem(pairs),
+        sem(pairs), sem(pairs), sem(pairs, targets), sem(pairs, targets), sem(pairs, targets), sem(pairs, targets),
+        sem(pairs), sem(pairs),
+    ]
+    hbm = pl.BlockSpec(memory_space=pltpu.HBM)
+    out = pl.pallas_call(
+        functools.partial(fused_kernel, (parts, slab, rows, depth, pairs, part)),
+        out_shape=pltpu.VMEM((tall, nx), f32),
+        in_specs=[hbm, pl.BlockSpec(memory_space=pltpu.SMEM)] + [hbm] * 6,
+        out_specs=pl.BlockSpec(memory_space=pltpu.VMEM),
+        scratch_shapes=scratch,
+        compiler_params=pltpu.CompilerParams(
+            collective_id=0, has_side_effects=True, vmem_limit_bytes=60 * 1024 * 1024
+        ),
+    )(source.reshape(tall, nx), cell_width, *(jnp.asarray(t) for t in consts))
+    return out.reshape(slab, rows, nx)
+
+
+def fits(source, parts, blocks):
+    slab, rows, nx = source.shape
+    return (
+        blocks == 4 and parts == 8 and nx % 256 == 0 and slab == 8 and rows % 16 == 0
+        and (rows * parts) % 256 == 0
+    )
+
+
+def per_device(source, cell_width):
+    if fits(source, lax.axis_size("pa"), lax.axis_size("gz")):
+        return fused(source, cell_width)
+    return on_device(source, cell_width)
+
+
 def solution(mesh):
     in_specs = (P("gz", "pa", None), P("gz"))
     out_specs = P("gz", "pa", None)
     return jax.shard_map(
-        on_device, mesh=mesh, in_specs=in_specs, out_specs=out_specs, check_vma=False
+        per_device, mesh=mesh, in_specs=in_specs, out_specs=out_specs, check_vma=False
     )

time: 249 us -> 34.2 us (0.14)
  blocking collectives: 94.1 us -> 0 us
  waiting for transfers between devices: 66.4 us -> 0 us
  local copies, waits for them, and re-layouts: 33 us -> 1.41 us
  matrix products: 24.9 us -> 0 us
  Pallas kernels: 12.9 us -> 32.7 us
  starting transfers between devices: 11.1 us -> 0 us
  other arithmetic: 5.18 us -> 0 us
    all_to_all x2 -> x0, blocking collectives: 87.4 us -> none  [the longest x1 74.4 us: on_device(): lax.all_to_all(along_y, 'pa', split_axis=2, concat_axis=1, tiled=True)]
    all_to_all x2 -> x0, waiting for transfers between devices: 66.4 us -> none  [the longest x1 58.5 us: on_device(): lax.all_to_all(along_x, 'pa', split_axis=1, concat_axis=2, tiled=True)]
    dot_general x4 -> x0, matrix products: 24.9 us -> none  [the longest x1 6.87 us: on_device(): along_y = jnp.einsum('zkl,lj->zkj', solved, sin_table, precision=HIGH)]
    pallas_call x3 -> x1, Pallas kernels: 12.9 us -> 32.7 us  [fused(): pl.pallas_call(functools.partial(fused_kernel, (parts, slab, rows, depth,...]
    all_to_all x6 -> x0, local copies, waits for them, and re-layouts: 19.4 us -> none  [the longest x2 9.79 us: on_device(): lax.all_to_all(along_x, 'pa', split_axis=1, concat_axis=2, tiled=True)]
    all_to_all x2 -> x0, starting transfers between devices: 11.1 us -> none  [the longest x1 7.43 us: on_device(): lax.all_to_all(along_x, 'pa', split_axis=1, concat_axis=2, tiled=True)]
    unnamed x1 -> x0, blocking collectives: 6.7 us -> none
    mul x3 -> x0, other arithmetic: 5.07 us -> none  [the longest x2 3.26 us: cosine_table(): return weights * summed_angles(width, a, b, False)]
  transfers between devices with their start and end apart: 2 -> 0, of which waited for: 2 -> 0; matrix products, arithmetic and copies ran while one was open for 3% -> 0% of each run, Pallas kernels for 0% -> 0%
where the time goes in v2:
time: 34.2 us; the launch traced here: 34.1 us
  Pallas kernels  32.7 us (96%)
  local copies, waits for them, and re-layouts  1.41 us (4%)
    pallas_call x1, Pallas kernels, fused(): pl.pallas_call(functools.partial(fused_kernel, (parts, slab, rows, depth,...  32.7 us
    unnamed x1, local copies, waits for them, and re-layouts  1.41 us

profile of v2, /device:TPU:0, one launch (start us, length us, event | category | flops | bytes accessed | tf_op | source)
XLA Modules:
  0.0 34.1 jit_solution(2347367918384414818)
XLA Ops:
  0.0 32.7 %shard_map.82 = f32[768,768]{1,0:T(8,128)S(1)} custom-call(f32[768,768]{1,0:T(8,128)} %bitcast.3, f32[8]{0:T(128)} %width.1, bf16[2,768,768]{2,1,0:T(8,128)(2,1)} %constant.12.clone.cos, bf16[3,2,192,192]{3,2,1,0:T(8,128)(2,1)} %constant.13.clone.phi, f32[3,96,128]{2,1,0:T(8,128)} %constant.14.clone.edge, f32[8,128]{1,0:T(8,128)} %constant.15.clone.lam, ...), custom_call_target="tpu_custom_call" | custom-call | tf_op jit(solution)/shard_map/pallas_call | solution.py:624
  32.7 1.4 %copy.10 = f32[8,96,768]{2,1,0:T(8,128)} copy(f32[8,96,768]{2,1,0:T(8,128)S(1)} %bitcast.2) | data formatting | bytes 4718592

commit v3 on v2

--- a/solution.py
+++ b/solution.py
@@ -237,7 +237,12 @@
     else:
         angle = (2 * l + 1) * np.pi / (2 * rows + 1)
         vectors = 2.0 / np.sqrt(2 * rows + 1) * np.sin(angle * (j + 1))
-    return vectors if kind < 2 else vectors[:, ::-1], 4.0 * np.sin(angle[:, 0] / 2) ** 2
+    order = np.concatenate([j[::2], j[1::2]])
+    vectors, values = vectors[order], 4.0 * np.sin(angle[order, 0] / 2) ** 2
+    if kind == 2:
+        vectors = vectors[:, ::-1]
+    edge = vectors[:, 0] if kind else vectors[:, -1] * np.where(np.arange(rows) < rows // 2, 1.0, -1.0)
+    return vectors, values, edge
 
 
 def stacked(table):
@@ -254,9 +259,9 @@
     rows = height // parts
     phi, edge = [], np.zeros((3, rows, 128), np.float32)
     for kind in range(3):
-        vectors, values = block_modes(rows, kind)
+        vectors, values, ends = block_modes(rows, kind)
         phi.append(np.stack([stacked(vectors), stacked(vectors.T)]))
-        edge[kind, :, 0], edge[kind, :, 1], edge[kind, :, 2] = values, vectors[:, 0], vectors[:, -1]
+        edge[kind, :, 0], edge[kind, :, 1] = values, ends
     lam = (4.0 * np.sin(np.arange(width) * np.pi / (2 * width)) ** 2).astype(np.float32).reshape(-1, 128)
     groups = lam.shape[0]
     targets = 2 * parts
@@ -274,8 +279,8 @@
 
 def fused_kernel(
     size, src, width, cos, phi, edge, lam, lam_t, modes, out,
-    sbuf, s16, ctab, ptab, etab, ltab, lttab, mtab, wbuf, cf, bc, xb, rx, fh, inv, vv,
-    inv2, cmine, cpeer, join, amine, apeer, eb, et, rb, gt, mb, ginv, gv, msg, rb2, e2, uo, xo,
+    sbuf, s16, ctab, ptab, etab, ltab, lttab, mtab, wbuf, cf, bc, xb, rx, fh, inv, vv, ratio,
+    ratio2, cmine, cpeer, join, ends2, amine, apeer, eb, et, rb, gt, mb, ginv, gratio, gv, msg, rb2, e2, uo, xo,
     in_sem, src_sem, cos_sem, w_send, w_recv, d_send, d_recv, a_send, a_recv,
     x_send, x_recv, y_send, y_recv, u_send, u_recv,
 ):
@@ -290,7 +295,7 @@
     kind = jnp.where(p == 0, 0, jnp.where(p == parts - 1, 2, 1))
     twin = {"gz": 2 * h + 1 - c}
     across = {"gz": 2 * (1 - h) + c}
-    at = lambda t: {"pa": lax.div(t, 2), "gz": 2 * lax.rem(t, 2) + c}
+    at = lambda t: {"pa": lax.div(t, 2), "gz": 2 * lax.rem(t, 2) + 1 - c}
 
     def remote(source, target, send, recv, device):
         return pltpu.make_async_remote_copy(
@@ -314,15 +319,12 @@
     load_cos(0).start()
     for load in loads:
         load.start()
-    for j in range(1, pairs):
-        load_cos(j).start()
     for z in range(slab):
         wbuf[g, z : z + 1, :] = jnp.full((1, 128), width[z], jnp.float32)
 
     barrier = pltpu.get_barrier_semaphore()
-    pl.semaphore_signal(barrier, inc=1, device_id=twin, device_id_type=MESH)
-    pl.semaphore_signal(barrier, inc=1, device_id={"gz": 2 * (1 - h) + 1 - c}, device_id_type=MESH)
-    for n in range(1, targets):
+    pl.semaphore_signal(barrier, inc=1, device_id=across, device_id_type=MESH)
+    for n in range(targets):
         pl.semaphore_signal(barrier, inc=1, device_id=at(lax.rem(me + n, targets)), device_id_type=MESH)
     pl.semaphore_wait(barrier, targets + 1)
 
@@ -332,6 +334,9 @@
 
     for n in range(SOURCE_PIECES):
         load_src(n).wait()
+        if n == SOURCE_PIECES - 1:
+            for j in range(1, pairs):
+                load_cos(j).start()
         r = slice(quarter * n, quarter * (n + 1))
         s16[0, r, :], s16[1, r, :] = halves(sbuf[r, :])
 
@@ -340,9 +345,9 @@
     swap_u = lambda j, who: remote(uo.at[j], xo.at[2 * j + who], u_send.at[j], u_recv.at[j], twin)
     piece = lambda t: pl.ds(pl.multiple_of(part * t, part), part)
     send_x = lambda j, n, t, who: remote(
-        et.at[j, piece(t), :], rb.at[j, who], x_send.at[j, n - 1], x_recv.at[j, who], at(t)
+        et.at[j, piece(t), :], rb.at[j, who], x_send.at[j, n], x_recv.at[j, who], at(t)
     )
-    send_y = lambda j, n, t, who: remote(msg.at[j, lax.div(t, 2)], rb2.at[j, who], y_send.at[j, n - 1], y_recv.at[j, who], at(t))
+    send_y = lambda j, n, t, who: remote(msg.at[j, lax.div(t, 2)], rb2.at[j, who], y_send.at[j, n], y_recv.at[j, who], at(t))
     peer_of = lambda n: lax.rem(me + n, targets)
     zero = jnp.zeros((part, 128), jnp.float32)
     lane = lax.broadcasted_iota(jnp.int32, (part, 128), 1)
@@ -373,7 +378,7 @@
         cf[2] = w
         for load in loads:
             load.wait()
-        for n in range(3):
+        for n in range(2):
             bc[n] = jnp.broadcast_to(etab[:, n : n + 1], (rows, 128))
         for n in range(half + 2):
             mb[n] = jnp.broadcast_to(mtab[n : n + 1, :], (8, mtab.shape[1]))
@@ -391,11 +396,14 @@
         eigen = bc[0] + ltab[pl.ds(2 * j + c, 1), :]
         ratios = [jnp.zeros((rows, 128), jnp.float32)] * 2
         for zz in range(depth):
-            for n, (side, keep) in enumerate([(h, inv), (1 - h, inv2)]):
+            for n, (side, keep) in enumerate([(h, ratio), (1 - h, ratio2)]):
                 zc, _z, outer, inner, w = cell(zz, side)
                 inverse = 1.0 / ((outer + inner) + w * eigen - outer * ratios[n])
-                keep[j, zc] = inverse
                 ratios[n] = inner * inverse
+                keep[j, zc] = ratios[n]
+                if n == 0:
+                    inv[j, zc] = inverse
+        ends2[j] = inverse
         cmine[j], cpeer[j] = ratios
         join[j] = 1.0 / (1.0 - ratios[0] * ratios[1])
         for n in range(2):
@@ -405,12 +413,16 @@
                 a, b = (slice(rows * y, rows * (y + 1)) for y in (zl, zl + 1))
                 block = rx.at[j] if n else xb.at[2 * j + c]
                 zc = slab * ((1 - c) if n else c) + zl
-                fh[j, zc], fh[j, zc + 1] = transform(0, block[a, :], block[b, :])
-        value = jnp.zeros((rows, 128), jnp.float32)
+                z = depth * h + zc
+                a, b = transform(0, block[a, :], block[b, :])
+                fh[j, zc] = cf[2, pl.ds(z, 1), :] * a
+                fh[j, zc + 1] = cf[2, pl.ds(z + 1, 1), :] * b
         for zz in range(depth):
-            zc, _z, outer, _inner, w = cell(zz, h)
-            value = (w * fh[j, zc] + outer * value) * inv[j, zc]
+            zc = cell(zz, h)[0]
+            value = fh[j, zc] + ratio[j, before] * value if zz else fh[j, zc]
             vv[j, zc] = value
+            before = zc
+        value = value * inv[j, before]
         amine[j] = value
         swap_a(j).start()
 
@@ -418,22 +430,23 @@
         x = amine[j] * join[j]
         y = cpeer[j] * x
         for zz in reversed(range(depth)):
-            zc, z, _outer, inner, _w = cell(zz, h)
-            yc, yz, _outer, across_in, _w = cell(zz, 1 - h)
+            zc, z = cell(zz, h)[:2]
+            yc, yz = cell(zz, 1 - h)[:2]
             if zz < depth - 1:
-                x = vv[j, zc] + inner * inv[j, zc] * x
-                y = across_in * inv2[j, yc] * y
-            for n in range(2):
-                eb[pl.ds(2 * depth * n + z, 1), :] = jnp.sum(bc[1 + n] * x, axis=0, keepdims=True)
-                eb[pl.ds(2 * depth * n + yz, 1), :] = jnp.sum(bc[1 + n] * y, axis=0, keepdims=True)
+                x = vv[j, zc] * inv[j, zc] + ratio[j, zc] * x
+                y = ratio2[j, yc] * y
+            for at_z, plane in ((z, x), (yz, y)):
+                weighted = bc[1] * plane
+                for n in range(2):
+                    rows_n = weighted[rows // 2 * n : rows // 2 * (n + 1)]
+                    eb[pl.ds(2 * depth * n + at_z, 1), :] = jnp.sum(rows_n, axis=0, keepdims=True)
         et[j] = jnp.transpose(eb[...])[:, :lanes]
-        for n in range(1, targets):
+        for n in range(targets):
             send_x(j, n, peer_of(n), me).start()
-        rb[j, me] = et[j, piece(me), :]
 
     def cut_factors():
         eigen_k = [
-            jnp.broadcast_to(jnp.sum(jnp.where(lane == 2 * j + c, lttab[...], 0.0), axis=1, keepdims=True), (part, 128))
+            jnp.broadcast_to(jnp.sum(jnp.where(lane == 2 * j + 1 - c, lttab[...], 0.0), axis=1, keepdims=True), (part, 128))
             for j in range(pairs)
         ]
 
@@ -447,6 +460,7 @@
                     inverse = 1.0 / ((lower + upper) + w * (eigen_k[j] + mb[0, :, col]) - lower * ratio[j * tiles + q])
                     ginv[j, z, :, col] = inverse
                     after.append(upper * inverse)
+                    gratio[j, z, :, col] = after[-1]
             return tuple(after)
 
         lax.fori_loop(0, total, cut_factor, (zero,) * (pairs * tiles))
@@ -474,35 +488,35 @@
     mode = lambda m: 1 + (m if m < half else m - half)
 
     def cut(j, carry):
-        for n in range(1, targets):
+        for n in range(targets):
             t = peer_of(n)
             send_x(j, n, t, t).wait_recv()
         edge = [rb[j, 2 * i] + rb[j, 2 * i + 1] for i in range(parts)]
-        jump = [edge[i][:, 2 * depth :] - edge[i + 1][:, : 2 * depth] for i in range(cuts)]
+        even, odd = ([e[:, k : k + 2 * depth] for e in edge] for k in (0, 2 * depth))
+        jump = [(even[i] - even[i + 1]) - (odd[i] + odd[i + 1]) for i in range(cuts)]
         mixed = [jump[i] - jump[cuts - 1 - i] for i in range(half)]
         mixed += [jump[i] + jump[cuts - 1 - i] for i in range(half)] + [jump[half]]
         for i in range(cuts):
             gt[i, :, : 2 * depth] = jump[i]
         value = [zero] * tiles
         for z in range(total):
-            lower, w = cf[0, z : z + 1, :], cf[2, z : z + 1, :]
+            w = cf[2, z : z + 1, :]
             force = [w * jnp.broadcast_to(m[:, z : z + 1], (part, 128)) for m in mixed]
             for q in range(tiles):
                 col = slice(128 * q, 128 * q + 128)
-                rhs = lower * value[q]
+                rhs = gratio[j, z - 1, :, col] * value[q] if z else zero
                 for m in terms(q):
                     rhs = rhs + force[m] * mb[mode(m), :, col]
-                value[q] = rhs * ginv[j, z, :, col]
-                gv[z, :, col] = value[q]
+                value[q] = rhs
+                gv[z, :, col] = rhs
 
         x = [zero] * tiles
         sums = [zero] * cuts
         for z in reversed(range(total)):
-            upper = cf[1, z : z + 1, :]
             along = [zero] * cuts
             for q in range(tiles):
                 col = slice(128 * q, 128 * q + 128)
-                x[q] = gv[z, :, col] + upper * ginv[j, z, :, col] * x[q]
+                x[q] = gv[z, :, col] * ginv[j, z, :, col] + gratio[j, z, :, col] * x[q]
                 for m in terms(q):
                     along[m] = along[m] + mb[mode(m), :, col] * x[q]
             for m in range(cuts):
@@ -514,38 +528,40 @@
         true[half] = gt[half] - sums[cuts - 1]
         for q in range(parts):
             left = true[q - 1] if q else zero
-            right = pltpu.roll(true[q], 2 * depth, 1) if q < parts - 1 else zero
-            msg[j, q] = (left + right)[:, :lanes]
-        for n in range(1, targets):
+            right = true[q] if q < parts - 1 else zero
+            msg[j, q] = ((left - right) + pltpu.roll(left + right, 2 * depth, 1))[:, :lanes]
+        for n in range(targets):
             send_y(j, n, peer_of(n), me).start()
-        rb2[j, me] = msg[j, p]
         return carry
 
     gt[...] = jnp.zeros(gt.shape, jnp.float32)
     lax.fori_loop(0, pairs, cut, 0)
 
     def second(j):
-        for n in range(1, targets):
+        for n in range(targets):
             t = peer_of(n)
             send_y(j, n, t, t).wait_recv()
         e2[...] = jnp.transpose(rb2[j].reshape(128, lanes))
-        value = jnp.zeros((rows, 128), jnp.float32)
-        other = value
+        def pull(z, w):
+            mode_rows = [slice(rows // 2 * n, rows // 2 * (n + 1)) for n in range(2)]
+            return jnp.concatenate([bc[1, r] * (w * e2[pl.ds(2 * depth * n + z, 1), :]) for n, r in enumerate(mode_rows)])
+
         for zz in range(depth):
-            zc, z, outer, _inner, w = cell(zz, h)
-            left, right = e2[pl.ds(z, 1), :], e2[pl.ds(2 * depth + z, 1), :]
-            force = fh[j, zc] + bc[1] * left - bc[2] * right
-            value = (w * force + outer * value) * inv[j, zc]
+            zc, z, _outer, _inner, w = cell(zz, h)
+            force = fh[j, zc] + pull(z, w)
+            value = force + ratio[j, before] * value if zz else force
             vv[j, zc] = value
-            zc, z, outer, _inner, w = cell(zz, 1 - h)
-            left, right = e2[pl.ds(z, 1), :], e2[pl.ds(2 * depth + z, 1), :]
-            other = (w * (bc[1] * left - bc[2] * right) + outer * other) * inv2[j, zc]
+            before = zc
+            zc, z, _outer, _inner, w = cell(zz, 1 - h)
+            force = pull(z, w)
+            other = force + ratio2[j, before2] * other if zz else force
+            before2 = zc
         swap_a(j).wait_recv()
-        x = (value + cmine[j] * (apeer[j] + other)) * join[j]
+        x = (value * inv[j, before] + cmine[j] * (apeer[j] + other * ends2[j])) * join[j]
         for zz in reversed(range(depth)):
-            zc, _z, _outer, inner, _w = cell(zz, h)
+            zc = cell(zz, h)[0]
             if zz < depth - 1:
-                x = vv[j, zc] + inner * inv[j, zc] * x
+                x = vv[j, zc] * inv[j, zc] + ratio[j, zc] * x
             fh[j, zc] = x
         for n in range(2):
             for zl in range(0, slab, 2):
@@ -584,7 +600,7 @@
     for n in range(1, 4):
         widths(n, g).wait_send()
     for j in range(pairs):
-        for n in range(1, targets):
+        for n in range(targets):
             send_x(j, n, peer_of(n), me).wait_send()
             send_y(j, n, peer_of(n), me).wait_send()
         swap(j).wait_send()
@@ -609,11 +625,11 @@
     scratch = [
         V((tall, nx), f32), V((2, tall, nx), b16), V((2, nx, nx), b16), V((2, 2 * rows, 2 * rows), b16), V((rows, 128), f32),
         V(consts[3].shape, f32), V((part, 128), f32), V(consts[5].shape, f32), V((4, slab, 128), f32),
-        V((3, 4 * slab, 128), f32), V((3, rows, 128), f32),
-        V((2 * pairs, tall, 128), f32), V((pairs, tall, 128), f32), V(lines, f32), V(lines, f32), V(lines, f32),
-        V(lines, f32), V(plane, f32), V(plane, f32), V(plane, f32), V(plane, f32), V(plane, f32),
+        V((3, 4 * slab, 128), f32), V((2, rows, 128), f32),
+        V((2 * pairs, tall, 128), f32), V((pairs, tall, 128), f32), V(lines, f32), V(lines, f32), V(lines, f32), V(lines, f32),
+        V(lines, f32), V(plane, f32), V(plane, f32), V(plane, f32), V(plane, f32), V(plane, f32), V(plane, f32),
         V((128, 128), f32), V((pairs, 128, lanes), f32), V(small, f32), V((parts, part, 128), f32),
-        V((parts // 2 + 1, 8, ny), f32), V((pairs, 2 * depth, part, ny), f32), V((2 * depth, part, ny), f32),
+        V((parts // 2 + 1, 8, ny), f32), V((pairs, 2 * depth, part, ny), f32), V((pairs, 2 * depth, part, ny), f32), V((2 * depth, part, ny), f32),
         V((pairs, parts, part, lanes), f32), V(small, f32), V((lanes, 128), f32),
         V((pairs, tall, 128), f32), V((2 * pairs, tall, 128), f32),
         sem(5), sem(SOURCE_PIECES), sem(pairs), sem(3), sem(4), sem(pairs), sem(pairs),

time: 34.2 us -> 32.9 us (0.962)
  Pallas kernels: 32.7 us -> 31.4 us
    pallas_call x1, Pallas kernels: 32.7 us -> 31.4 us  [fused(): pl.pallas_call(functools.partial(fused_kernel, (parts, slab, rows, depth,...]
where the time goes in v3:
time: 32.9 us; the launch traced here: 32.8 us
  Pallas kernels  31.4 us (95%)
  local copies, waits for them, and re-layouts  1.41 us (4%)
    pallas_call x1, Pallas kernels, fused(): pl.pallas_call(functools.partial(fused_kernel, (parts, slab, rows, depth,...  31.4 us
    unnamed x1, local copies, waits for them, and re-layouts  1.41 us

profile of v3, /device:TPU:0, one launch (start us, length us, event | category | flops | bytes accessed | tf_op | source)
XLA Modules:
  0.0 32.8 jit_solution(6749657692235156370)
XLA Ops:
  0.0 31.4 %shard_map.82 = f32[768,768]{1,0:T(8,128)S(1)} custom-call(f32[768,768]{1,0:T(8,128)} %bitcast.3, f32[8]{0:T(128)} %width.1, bf16[2,768,768]{2,1,0:T(8,128)(2,1)} %constant.12.clone.cos, bf16[3,2,192,192]{3,2,1,0:T(8,128)(2,1)} %constant.13.clone.phi, f32[3,96,128]{2,1,0:T(8,128)} %constant.14.clone.edge, f32[8,128]{1,0:T(8,128)} %constant.15.clone.lam, ...), custom_call_target="tpu_custom_call" | custom-call | tf_op jit(solution)/shard_map/pallas_call | solution.py:640
  31.4 1.4 %copy.10 = f32[8,96,768]{2,1,0:T(8,128)} copy(f32[8,96,768]{2,1,0:T(8,128)S(1)} %bitcast.2) | data formatting | bytes 4718592

commit v4 on v3

--- a/solution.py
+++ b/solution.py
@@ -326,11 +326,7 @@
     pl.semaphore_signal(barrier, inc=1, device_id=across, device_id_type=MESH)
     for n in range(targets):
         pl.semaphore_signal(barrier, inc=1, device_id=at(lax.rem(me + n, targets)), device_id_type=MESH)
-    pl.semaphore_wait(barrier, targets + 1)
-
     widths = lambda n, who: remote(wbuf.at[who], wbuf.at[who], w_send.at[n - 1], w_recv.at[who], {"gz": lax.rem(g + n, 4)})
-    for n in range(1, 4):
-        widths(n, g).start()
 
     for n in range(SOURCE_PIECES):
         load_src(n).wait()
@@ -359,14 +355,6 @@
         z = depth * side + zc
         row = pl.ds(z, 1)
         return zc, z, cf[side, row, :], cf[1 - side, row, :], cf[2, row, :]
-
-    def along_x(j):
-        load_cos(j).wait()
-        dot = lambda a, b: lax.dot_general(s16[a], ctab[b, group(j), :], NT, preferred_element_type=jnp.float32)
-        product = dot(0, 0) + dot(1, 0) + dot(0, 1)
-        xb[2 * j] = product[:, :128]
-        xb[2 * j + 1] = product[:, 128:]
-        swap(j).start()
 
     def coefficients():
         for n in range(1, 4):
@@ -392,7 +380,7 @@
         both = both[:rows] + both[rows:]
         return both[:, :128], both[:, 128:]
 
-    def first(j):
+    def factor(j):
         eigen = bc[0] + ltab[pl.ds(2 * j + c, 1), :]
         ratios = [jnp.zeros((rows, 128), jnp.float32)] * 2
         for zz in range(depth):
@@ -406,6 +394,15 @@
         ends2[j] = inverse
         cmine[j], cpeer[j] = ratios
         join[j] = 1.0 / (1.0 - ratios[0] * ratios[1])
+
+    def along_x(j):
+        load_cos(j).wait()
+        dot = lambda a, b: lax.dot_general(s16[a], ctab[b, group(j), :], NT, preferred_element_type=jnp.float32)
+        product = dot(0, 0) + dot(1, 0) + dot(0, 1)
+        xb[2 * j] = product[:, :128]
+        xb[2 * j + 1] = product[:, 128:]
+
+    def first(j):
         for n in range(2):
             if n:
                 swap(j).wait_recv()
@@ -465,23 +462,30 @@
 
         lax.fori_loop(0, total, cut_factor, (zero,) * (pairs * tiles))
 
-    def head(step, carry):
-        @pl.when(step < pairs)
-        def _():
-            along_x(step)
-
-        @pl.when(step == 1)
-        def _():
-            coefficients()
-
-        @pl.when(step >= 1)
-        def _():
-            first(step - 1)
-            first_back(step - 1)
-
+    ahead = 1
+    for j in range(ahead):
+        along_x(j)
+    pl.semaphore_wait(barrier, targets + 1)
+    for n in range(1, 4):
+        widths(n, g).start()
+    for j in range(ahead):
+        swap(j).start()
+
+    def start_x(j, carry):
+        along_x(j)
+        swap(j).start()
         return carry
 
-    lax.fori_loop(0, pairs + 1, head, 0)
+    lax.fori_loop(ahead, pairs, start_x, 0)
+    coefficients()
+
+    def blocks(j, carry):
+        factor(j)
+        first(j)
+        first_back(j)
+        return carry
+
+    lax.fori_loop(0, pairs, blocks, 0)
     cut_factors()
 
     terms = lambda q: range(half) if q < tiles // 2 else range(half, cuts)

time: 32.9 us -> 31.6 us (0.960)
  Pallas kernels: 31.4 us -> 30.1 us
    pallas_call x1, Pallas kernels: 31.4 us -> 30.1 us  [fused(): pl.pallas_call(functools.partial(fused_kernel, (parts, slab, rows, depth,...]
where the time goes in v4:
time: 31.6 us; the launch traced here: 31.5 us
  Pallas kernels  30.1 us (95%)
  local copies, waits for them, and re-layouts  1.41 us (4%)
    pallas_call x1, Pallas kernels, fused(): pl.pallas_call(functools.partial(fused_kernel, (parts, slab, rows, depth,...  30.1 us
    unnamed x1, local copies, waits for them, and re-layouts  1.41 us

profile of v4, /device:TPU:0, one launch (start us, length us, event | category | flops | bytes accessed | tf_op | source)
XLA Modules:
  0.0 31.5 jit_solution(16302375455702210390)
XLA Ops:
  0.0 30.1 %shard_map.82 = f32[768,768]{1,0:T(8,128)S(1)} custom-call(f32[768,768]{1,0:T(8,128)} %bitcast.3, f32[8]{0:T(128)} %width.1, bf16[2,768,768]{2,1,0:T(8,128)(2,1)} %constant.12.clone.cos, bf16[3,2,192,192]{3,2,1,0:T(8,128)(2,1)} %constant.13.clone.phi, f32[3,96,128]{2,1,0:T(8,128)} %constant.14.clone.edge, f32[8,128]{1,0:T(8,128)} %constant.15.clone.lam, ...), custom_call_target="tpu_custom_call" | custom-call | tf_op jit(solution)/shard_map/pallas_call | solution.py:644
  30.1 1.4 %copy.10 = f32[8,96,768]{2,1,0:T(8,128)} copy(f32[8,96,768]{2,1,0:T(8,128)S(1)} %bitcast.2) | data formatting | bytes 4718592

commit v5 on v4

--- a/solution.py
+++ b/solution.py
@@ -314,11 +314,11 @@
             [(phi.at[kind], ptab), (edge.at[kind], etab), (lam, ltab), (lam_t.at[me], lttab), (modes, mtab)]
         )
     ]
+    for load in loads:
+        load.start()
     for n in range(SOURCE_PIECES):
         load_src(n).start()
     load_cos(0).start()
-    for load in loads:
-        load.start()
     for z in range(slab):
         wbuf[g, z : z + 1, :] = jnp.full((1, 128), width[z], jnp.float32)
 
@@ -327,6 +327,16 @@
     for n in range(targets):
         pl.semaphore_signal(barrier, inc=1, device_id=at(lax.rem(me + n, targets)), device_id_type=MESH)
     widths = lambda n, who: remote(wbuf.at[who], wbuf.at[who], w_send.at[n - 1], w_recv.at[who], {"gz": lax.rem(g + n, 4)})
+
+    out[...] = jnp.zeros(out.shape, jnp.float32)
+    gt[...] = jnp.zeros(gt.shape, jnp.float32)
+    for load in loads:
+        load.wait()
+    for n in range(2):
+        bc[n] = jnp.broadcast_to(etab[:, n : n + 1], (rows, 128))
+    for n in range(half + 2):
+        mb[n] = jnp.broadcast_to(mtab[n : n + 1, :], (8, mtab.shape[1]))
+    eb[lanes:, :] = jnp.zeros((128 - lanes, 128), jnp.float32)
 
     for n in range(SOURCE_PIECES):
         load_src(n).wait()
@@ -364,13 +374,6 @@
         cf[0] = 2.0 / (w + jnp.where(z == 0, 0.0, pltpu.roll(w, 1, 0)))
         cf[1] = 2.0 / (w + jnp.where(z == total - 1, 0.0, pltpu.roll(w, total - 1, 0)))
         cf[2] = w
-        for load in loads:
-            load.wait()
-        for n in range(2):
-            bc[n] = jnp.broadcast_to(etab[:, n : n + 1], (rows, 128))
-        for n in range(half + 2):
-            mb[n] = jnp.broadcast_to(mtab[n : n + 1, :], (8, mtab.shape[1]))
-        eb[lanes:, :] = jnp.zeros((128 - lanes, 128), jnp.float32)
 
     def transform(which, a, b):
         hi, lo = halves(jnp.concatenate([a, b], axis=1))
@@ -397,8 +400,11 @@
 
     def along_x(j):
         load_cos(j).wait()
-        dot = lambda a, b: lax.dot_general(s16[a], ctab[b, group(j), :], NT, preferred_element_type=jnp.float32)
-        product = dot(0, 0) + dot(1, 0) + dot(0, 1)
+        table = [ctab[n, group(j), :] for n in range(2)]
+        product = lax.dot_general(
+            jnp.concatenate([s16[0], s16[1], s16[0]], axis=1), jnp.concatenate([table[0], table[0], table[1]], axis=1),
+            NT, preferred_element_type=jnp.float32,
+        )
         xb[2 * j] = product[:, :128]
         xb[2 * j + 1] = product[:, 128:]
 
@@ -538,7 +544,6 @@
             send_y(j, n, peer_of(n), me).start()
         return carry
 
-    gt[...] = jnp.zeros(gt.shape, jnp.float32)
     lax.fori_loop(0, pairs, cut, 0)
 
     def second(j):
@@ -582,10 +587,12 @@
             s16[0, :, 128 * n : 128 * n + 128], s16[1, :, 128 * n : 128 * n + 128] = halves(xo[2 * j + n])
         for n in range(pairs):
             i = slice(wide * n, wide * (n + 1))
-            dot = lambda a, b: lax.dot_general(
-                s16[a, :, :wide], ctab[b, group(j), i], NN, preferred_element_type=jnp.float32
+            hi, lo = s16[0, :, :wide], s16[1, :, :wide]
+            table = [ctab[m, group(j), i] for m in range(2)]
+            out[:, i] = out[:, i] + lax.dot_general(
+                jnp.concatenate([hi, lo, hi], axis=1), jnp.concatenate([table[0], table[0], table[1]], axis=0),
+                NN, preferred_element_type=jnp.float32,
             )
-            out[:, i] = out[:, i] + (dot(0, 0) + dot(1, 0) + dot(0, 1))
 
     def tail(step, carry):
         @pl.when(step < pairs)
@@ -598,7 +605,6 @@
 
         return carry
 
-    out[...] = jnp.zeros(out.shape, jnp.float32)
     lax.fori_loop(0, pairs + 1, tail, 0)
 
     for n in range(1, 4):

time: 31.6 us -> 31.5 us (level)
  no operation moved by 1% of the time
where the time goes in v5:
time: 31.5 us; the launch traced here: 31.4 us
  Pallas kernels  29.9 us (95%)
  local copies, waits for them, and re-layouts  1.41 us (4%)
    pallas_call x1, Pallas kernels, fused(): pl.pallas_call(functools.partial(fused_kernel, (parts, slab, rows, depth,...  29.9 us
    unnamed x1, local copies, waits for them, and re-layouts  1.41 us

profile of v5, /device:TPU:0, one launch (start us, length us, event | category | flops | bytes accessed | tf_op | source)
XLA Modules:
  0.0 31.4 jit_solution(358949481659663595)
XLA Ops:
  0.0 29.9 %shard_map.82 = f32[768,768]{1,0:T(8,128)S(1)} custom-call(f32[768,768]{1,0:T(8,128)} %bitcast.3, f32[8]{0:T(128)} %width.1, bf16[2,768,768]{2,1,0:T(8,128)(2,1)} %constant.12.clone.cos, bf16[3,2,192,192]{3,2,1,0:T(8,128)(2,1)} %constant.13.clone.phi, f32[3,96,128]{2,1,0:T(8,128)} %constant.14.clone.edge, f32[8,128]{1,0:T(8,128)} %constant.15.clone.lam, ...), custom_call_target="tpu_custom_call" | custom-call | tf_op jit(solution)/shard_map/pallas_call | solution.py:650
  30.0 1.4 %copy.10 = f32[8,96,768]{2,1,0:T(8,128)} copy(f32[8,96,768]{2,1,0:T(8,128)S(1)} %bitcast.2) | data formatting | bytes 4718592

commit v6 on v5

--- a/solution.py
+++ b/solution.py
@@ -354,7 +354,8 @@
         et.at[j, piece(t), :], rb.at[j, who], x_send.at[j, n], x_recv.at[j, who], at(t)
     )
     send_y = lambda j, n, t, who: remote(msg.at[j, lax.div(t, 2)], rb2.at[j, who], y_send.at[j, n], y_recv.at[j, who], at(t))
-    peer_of = lambda n: lax.rem(me + n, targets)
+    upper_half = lax.div(me, parts)
+    peer_of = lambda n: upper_half * n + (1 - upper_half) * (targets - 1 - n)
     zero = jnp.zeros((part, 128), jnp.float32)
     lane = lax.broadcasted_iota(jnp.int32, (part, 128), 1)
     total = 4 * slab

time: 31.5 us -> 31.6 us (level)
  no operation moved by 1% of the time
where the time goes in v6:
time: 31.6 us; the launch traced here: 31.4 us
  Pallas kernels  30 us (95%)
  local copies, waits for them, and re-layouts  1.41 us (4%)
    pallas_call x1, Pallas kernels, fused(): pl.pallas_call(functools.partial(fused_kernel, (parts, slab, rows, depth,...  30 us
    unnamed x1, local copies, waits for them, and re-layouts  1.41 us

profile of v6, /device:TPU:0, one launch (start us, length us, event | category | flops | bytes accessed | tf_op | source)
XLA Modules:
  0.0 31.4 jit_solution(14415812602490635113)
XLA Ops:
  0.0 30.0 %shard_map.82 = f32[768,768]{1,0:T(8,128)S(1)} custom-call(f32[768,768]{1,0:T(8,128)} %bitcast.3, f32[8]{0:T(128)} %width.1, bf16[2,768,768]{2,1,0:T(8,128)(2,1)} %constant.12.clone.cos, bf16[3,2,192,192]{3,2,1,0:T(8,128)(2,1)} %constant.13.clone.phi, f32[3,96,128]{2,1,0:T(8,128)} %constant.14.clone.edge, f32[8,128]{1,0:T(8,128)} %constant.15.clone.lam, ...), custom_call_target="tpu_custom_call" | custom-call | tf_op jit(solution)/shard_map/pallas_call | solution.py:651
  30.0 1.4 %copy.10 = f32[8,96,768]{2,1,0:T(8,128)} copy(f32[8,96,768]{2,1,0:T(8,128)S(1)} %bitcast.2) | data formatting | bytes 4718592
